TPU v7x, 512 devices: a whole 4x8x8 slice. The times are simulated.
512 devices in a mesh: grp: 2 (over core), row: 16 (over x, y_hi), col: 16 (over y_lo, z).
Axes of the slice: x: 4, y: 8 (y_hi: 4, y_lo: 2; y = y_hi * 2 + y_lo), z: 8, core: 2. Of those that a mesh axis runs over, the one named last changes fastest.
Arguments:
- front: float32 [16384, 16384], P(('grp', 'row'), 'col'), may hold values from -9 to 1400, as said below
- prev_lower: bfloat16 [16384, 256], P(('grp', 'row', 'col')), may hold values from -0.035888672 to 0.035888672
- prev_pivots: float32 [256], replicated, may hold values from 150 to 400
- pivot_order: int32 [2, 256], replicated, may hold values from 0 to 255, each once within a row
Outputs:
- schur: float32 [16384, 16384], P(('grp', 'row'), 'col')
- panels_scaled: float32 [16384, 512], P(('grp', 'row', 'col'))
- pivots: float32 [512], replicated
Inputs may be any that keep to these rules, and one draw needn't show every extreme that they name: front is symmetric and positive definite, and stays so after the update by the pending panel, so that every Schur complement of the window is positive definite. Each row of pivot_order names every number of 0 to 255 once.
All inputs are finite; a program needn't handle non-finite values.
Results may differ from a plain program's by a relative error of at most 0.0003.
Values may be sent and summed in bfloat16 or wider, within the bound.
A program may use at most 128 MiB of HBM per device.

v0:
```python
import jax
import jax.numpy as jnp
from jax import lax
from jax.sharding import PartitionSpec as P


def spread(array, axis, root):
    mine = lax.axis_index(axis) == root
    return lax.psum(jnp.where(mine, array, jnp.zeros_like(array)), axis)


def picked(array, axis, root):
    return lax.dynamic_index_in_dim(lax.all_gather(array, axis), root, 0, keepdims=False)


def in_order(tiles, dim):
    dims = list(tiles.shape[1:])
    dims[dim] *= tiles.shape[0]
    return jnp.moveaxis(tiles, 0, dim).reshape(dims)


def copy_for_each(array, axis):
    copies = jnp.broadcast_to(array, (lax.axis_size(axis), *array.shape))
    return lax.all_to_all(copies, axis, split_axis=0, concat_axis=0, tiled=True)


def gathered_copies(array, axis, dim):
    return in_order(copy_for_each(array, axis), dim)


def apply_panel(trailing, factor_rows, factor_cols, pivot_values):
    scaled = (factor_rows.astype(jnp.float32) * pivot_values).astype(jnp.bfloat16)
    update = lax.dot_general(
        scaled, factor_cols, (((1,), (1,)), ((), ())), preferred_element_type=jnp.float32
    )
    return trailing - update


def factor_panel(panel_cols, pivot_row, start, row_count, col_count):
    exact = lax.Precision.HIGHEST
    panel_width = panel_cols.shape[1]
    col_devices = lax.axis_size("col")
    row_owner = start // row_count
    col_owner = start // col_count
    row_start = start % row_count
    diagonal_block = panel_cols[row_start : row_start + panel_width]
    diagonal_block = spread(
        diagonal_block, ("grp", "row", "col"), row_owner * col_devices + col_owner
    )
    select = (pivot_row[:, None] == jnp.arange(panel_width, dtype=jnp.int32)[None, :]).astype(
        jnp.float32
    )
    permuted = jnp.dot(jnp.dot(select, diagonal_block, precision=exact), select.T, precision=exact)
    cholesky_factor = jnp.linalg.cholesky(permuted)
    root_diag = jnp.diagonal(cholesky_factor)
    moved = jnp.dot(panel_cols, select.T, precision=exact)
    solved = lax.linalg.triangular_solve(
        cholesky_factor, moved, left_side=False, lower=True, transpose_a=True
    )
    factor_rows = (solved / root_diag).astype(jnp.bfloat16)
    factor_rows = picked(factor_rows, "col", col_owner)
    return (factor_rows, root_diag * root_diag)


def column_rows(factor_rows, pair_count):
    pieces = [
        picked(factor_rows, ("grp", "row"), lax.axis_index("col") * pair_count + number)
        for number in range(pair_count)
    ]
    return jnp.concatenate(pieces, axis=0)


def body(front, prev_lower, prev_pivots, pivot_order):
    row_count, col_count = front.shape
    panel_width = prev_lower.shape[1]
    panel_count = pivot_order.shape[0]
    pair_count = col_count // row_count
    own_rows = prev_lower.shape[0]
    offset = lax.axis_index("col") * own_rows
    row_base = (lax.axis_index("grp") * lax.axis_size("row") + lax.axis_index("row")) * row_count
    rows_here = row_base + jnp.arange(row_count, dtype=jnp.int32)
    factor_rows = gathered_copies(prev_lower, "col", 0)
    factor_cols = column_rows(factor_rows, pair_count)
    pivot_values = prev_pivots
    trailing = front
    outputs = []
    pivot_list = []
    for panel_index in range(panel_count):
        start = panel_index * panel_width
        col_start = start % col_count
        col_end = col_start + panel_width
        middle = apply_panel(
            trailing[:, col_start:col_end],
            factor_rows,
            factor_cols[col_start:col_end],
            pivot_values,
        )
        new_rows, new_pivots = factor_panel(
            middle, pivot_order[panel_index], start, row_count, col_count
        )
        before = apply_panel(
            trailing[:, :col_start], factor_rows, factor_cols[:col_start], pivot_values
        )
        beyond = apply_panel(
            trailing[:, col_end:], factor_rows, factor_cols[col_end:], pivot_values
        )
        trailing = jnp.concatenate([before, middle, beyond], axis=1)
        empty_rows = jnp.zeros_like(new_rows)
        shown_rows = jnp.where((rows_here >= start)[:, None], new_rows, empty_rows)
        factor_rows = jnp.where((rows_here >= start + panel_width)[:, None], new_rows, empty_rows)
        pivot_values = new_pivots
        own_part = lax.dynamic_slice_in_dim(shown_rows, offset, own_rows, 0)
        outputs.append(own_part.astype(jnp.float32) * new_pivots)
        pivot_list.append(new_pivots)
        if panel_index + 1 < panel_count:
            factor_cols = column_rows(factor_rows, pair_count)
    return (trailing, jnp.concatenate(outputs, axis=1), jnp.concatenate(pivot_list))


def solution(mesh):
    in_specs = (P(("grp", "row"), "col"), P(("grp", "row", "col"), None), P(), P())
    out_specs = (P(("grp", "row"), "col"), P(("grp", "row", "col"), None), P())
    return jax.shard_map(body, mesh=mesh, in_specs=in_specs, out_specs=out_specs, check_vma=False)
```

profile of v0, /device:TPU:1, one launch (start us, length us, event | category | flops | bytes accessed | tf_op | source)
XLA Modules:
  0.0 1028.8 jit_solution(693259556230813058)
XLA Ops:
  8.0 20.2 %all_to_all.5 = bf16[16,32,256]{2,1,0:T(8,128)(2,1)} all-to-all(bf16[16,32,256]{2,1,0:T(8,128)(2,1)S(1)} %broadcast_in_dim.42), channel_id=1, replica_groups=mesh['grp'=2,'row'=16,'col'=16] {'col'}, dimensions={0} | all-to-all | bytes 524288 | tf_op jit(solution)/shard_map/all_to_all | solution.py:24
  29.2 79.1 %all-gather.7.cloned.1.call-done = bf16[32,512,256]{2,1,0:T(8,128)(2,1)} async-done(((bf16[1,512,256]{2,1,0:T(8,128)(2,1)}), bf16[32,512,256]{2,1,0:T(8,128)(2,1)}) %all-gather.7.cloned.1.call-update) | async-done | bytes 8388624 | tf_op jit(solution)/shard_map/all_gather | solution.py:13
  110.9 275.6 %all-reduce.4.cloned.1.call-done = f32[256,256]{0,1:T(8,128)} async-done(((f32[256,256]{0,1:T(8,128)}), f32[256,256]{0,1:T(8,128)}) %all-reduce.4.cloned.1.call-update) | async-done | bytes 262160 | tf_op jit(solution)/shard_map/psum | solution.py:9
  386.5 1.3 fusion.21
  388.4 11.7 %cholesky.130 = f32[128,128]{1,0:T(8,128)S(1)} custom-call(f32[128,128]{1,0:T(8,128)S(1)} %cholesky.194), custom_call_target="Cholesky" | custom-call | tf_op jit(solution)/shard_map/jit(cholesky)/cholesky | solution.py:54
  400.2 9.8 custom-call.17
  410.5 11.7 %cholesky.147 = f32[128,128]{1,0:T(8,128)S(1)} custom-call(f32[128,128]{1,0:T(8,128)S(1)} %convolution_subtract_fusion.8), custom_call_target="Cholesky" | custom-call | tf_op jit(solution)/shard_map/jit(cholesky)/cholesky | solution.py:54
  424.3 4.2 while.4
  425.1 1.4 bitcast_dynamic-update-slice_fusion.4
  427.1 1.4 bitcast_dynamic-update-slice_fusion.4
  428.5 19.7 %custom-call.18 = f32[2,128,128]{1,2,0:T(8,128)S(1)} custom-call(f32[2,128,128]{2,1,0:T(8,128)S(1)} %get-tuple-element.19), custom_call_target="InvertDiagBlocksLowerTriangular" | custom-call | tf_op jit(solution)/shard_map/triangular_solve/custom-call.0 | solution.py:57
  449.7 2.3 gather_fusion
  452.9 66.8 %all-gather.11.cloned.1.call-done = bf16[8192,256]{1,0:T(8,128)(2,1)} async-done(((bf16[512,256]{1,0:T(8,128)(2,1)}), bf16[8192,256]{1,0:T(8,128)(2,1)}) %all-gather.11.cloned.1.call-update) | async-done | bytes 4194320 | tf_op jit(solution)/shard_map/all_gather | solution.py:13
  519.7 1.8 bitcast_select_fusion
  521.6 1.6 copy.44
  523.3 1.2 dynamic-slice_bitcast_fusion.1
  524.8 1.5 convolution_subtract_fusion
  526.3 82.8 %all-gather.9.cloned.1.call-done = bf16[32,512,256]{2,1,0:T(8,128)(2,1)} async-done(((bf16[1,512,256]{2,1,0:T(8,128)(2,1)}), bf16[32,512,256]{2,1,0:T(8,128)(2,1)}) %all-gather.9.cloned.1.call-update) | async-done | bytes 8388624 | tf_op jit(solution)/shard_map/all_gather | solution.py:13
  609.1 1.4 convolution_subtract_fusion.2
  612.0 274.6 %all-reduce.6.cloned.1.call-done = f32[256,256]{0,1:T(8,128)} async-done(((f32[256,256]{0,1:T(8,128)}), f32[256,256]{0,1:T(8,128)}) %all-reduce.6.cloned.1.call-update) | async-done | bytes 262160 | tf_op jit(solution)/shard_map/psum | solution.py:9
  886.7 1.3 fusion.17
  888.6 11.7 %cholesky.164 = f32[128,128]{1,0:T(8,128)S(1)} custom-call(f32[128,128]{1,0:T(8,128)S(1)} %cholesky.197), custom_call_target="Cholesky" | custom-call | tf_op jit(solution)/shard_map/jit(cholesky)/cholesky | solution.py:54
  901.0 9.8 custom-call.19
  911.3 11.7 %cholesky.181 = f32[128,128]{1,0:T(8,128)S(1)} custom-call(f32[128,128]{1,0:T(8,128)S(1)} %convolution_subtract_fusion.7), custom_call_target="Cholesky" | custom-call | tf_op jit(solution)/shard_map/jit(cholesky)/cholesky | solution.py:54
  924.9 4.0 while.5
  925.8 1.3 bitcast_dynamic-update-slice_fusion.5
  927.7 1.3 bitcast_dynamic-update-slice_fusion.5
  929.0 19.7 %custom-call.20 = f32[2,128,128]{1,2,0:T(8,128)S(1)} custom-call(f32[2,128,128]{2,1,0:T(8,128)S(1)} %get-tuple-element.20), custom_call_target="InvertDiagBlocksLowerTriangular" | custom-call | tf_op jit(solution)/shard_map/triangular_solve/custom-call.0 | solution.py:57
  949.9 2.3 gather_fusion.1
  954.8 1.7 convolution_subtract_fusion.1
  956.6 1.8 copy.39
  959.0 61.2 %all-gather.13.cloned.1.call-done = bf16[8192,256]{1,0:T(8,128)(2,1)} async-done(((bf16[512,256]{1,0:T(8,128)(2,1)}), bf16[8192,256]{1,0:T(8,128)(2,1)}) %all-gather.13.cloned.1.call-update) | async-done | bytes 4194320 | tf_op jit(solution)/shard_map/all_gather | solution.py:13
  (97 shorter events, 21.5 us)
Async XLA Ops:
  7.2 21.1 %slice-start = ((f32[512,1024]{1,0:T(8,128)}), f32[512,256]{1,0:T(8,128)S(1)}, s32[]{:S(2)}) async-start(f32[512,1024]{1,0:T(8,128)} %param.7), calls=%async_computation.7 | async-start | bytes 1048576 | tf_op jit(solution)/shard_map/slice | solution.py:93
  7.2 21.4 %copy-start.4 = (s32[2,256]{1,0:T(2,128)S(1)}, s32[2,256]{1,0:T(2,128)}, u32[]{:S(2)}) copy-start(s32[2,256]{1,0:T(2,128)} %param.10) | copy-start | bytes 6148
  7.2 21.4 %copy-start.3 = (f32[256]{0:T(256)S(1)}, f32[256]{0:T(256)}, u32[]{:S(2)}) copy-start(f32[256]{0:T(256)} %param.9) | copy-start | bytes 3076
  7.2 101.1 %all-gather.7.cloned.1.call-start = ((), (), s32[]{:S(2)}) async-start(), calls=%async_computation.1 | async-start | bytes 8650752 | tf_op jit(solution)/shard_map/all_gather | solution.py:13
  28.2 1.0 copy-start.2
  28.2 358.2 %all-reduce.4.cloned.1.call-start = ((), (), s32[]{:S(2)}) async-start(), calls=%async_computation.2 | async-start | bytes 524288 | tf_op jit(solution)/shard_map/psum | solution.py:9
  110.2 409.5 %all-gather.11.cloned.1.call-start = ((), (), s32[]{:S(2)}) async-start(), calls=%async_computation.5 | async-start | bytes 4456448 | tf_op jit(solution)/shard_map/all_gather | solution.py:13
  452.8 68.8 %slice-start.1 = ((f32[512,1024]{1,0:T(8,128)}), f32[512,768]{1,0:T(8,128)S(1)}, s32[]{:S(2)}) async-start(f32[512,1024]{1,0:T(8,128)} %param.7), calls=%async_computation.8 | async-start | bytes 3145728 | tf_op jit(solution)/shard_map/slice | solution.py:105
  452.8 156.3 %all-gather.9.cloned.1.call-start = ((), (), s32[]{:S(2)}) async-start(), calls=%async_computation.3 | async-start | bytes 8650752 | tf_op jit(solution)/shard_map/all_gather | solution.py:13
  521.5 365.1 %all-reduce.6.cloned.1.call-start = ((), (), s32[]{:S(2)}) async-start(), calls=%async_computation.4 | async-start | bytes 524288 | tf_op jit(solution)/shard_map/psum | solution.py:9
  523.2 1.6 copy-start.1
  524.5 84.7 %copy-start = (bf16[1,512,256]{2,1,0:T(8,128)(2,1)S(1)}, bf16[1,512,256]{2,1,0:T(8,128)(2,1)}, u32[]{:S(2)}) copy-start(bf16[1,512,256]{2,1,0:T(8,128)(2,1)} %bitcast_select_fusion) | copy-start | bytes 786436
  611.3 408.9 %all-gather.13.cloned.1.call-start = ((), (), s32[]{:S(2)}) async-start(), calls=%async_computation.6 | async-start | bytes 4456448 | tf_op jit(solution)/shard_map/all_gather | solution.py:13
  949.7 3.8 slice-start.2
Sparse Core Ops, SparseCore 0:
  28.4 79.8 all-gather.6
  113.8 272.6 all-reduce.3
  453.0 66.7 all-gather.10
  522.7 86.3 all-gather.8
  614.0 272.6 all-reduce.5
  953.5 66.7 all-gather.12
where the time goes:
time: 1040 us; the launch traced here: 1030 us
  waiting for transfers between devices  840 us (81%)
  other arithmetic  114 us (11%)
  local copies, waits for them, and re-layouts  20.7 us (2%)
  blocking collectives  20.2 us (2%)
  between operations  17.1 us (2%)
  matrix products  15.4 us (1%)
    psum x2, waiting for transfers between devices, spread(): return lax.psum(jnp.where(mine, array, jnp.zeros_like(array)), axis)  550 us
    all_gather x4, waiting for transfers between devices, picked(): lax.all_gather(array, axis)  290 us
    another operation x13, other arithmetic, factor_panel(): cholesky_factor = jnp.linalg.cholesky(permuted)  68.5 us
    another operation x5, other arithmetic, factor_panel(): lax.linalg.triangular_solve(cholesky_factor, moved, left_side=False, lowe...  39.4 us
  transfers between devices with their start and end apart: 6, of which 6 were waited for; matrix products, arithmetic and copies ran while one was open for 1% of the time, Pallas kernels for 0%

commit v1 on v0

v1 whole, which is shorter than its diff:
```python
import jax
import jax.numpy as jnp
from jax import lax
from jax.experimental import pallas as pl
from jax.experimental.pallas import tpu as pltpu
from jax.sharding import PartitionSpec as P

F32 = jnp.float32
BF16 = jnp.bfloat16
EXACT = lax.Precision.HIGHEST
MESH = pl.DeviceIdType.MESH
CHUNK = 32
WIDTH = 256
HALF = 128
VMEM_LIMIT = 60 * 1024 * 1024


def place():
    return lax.axis_index("grp"), lax.axis_index("row"), lax.axis_index("col")


def remote(src, dst, send_sem, recv_sem, device):
    return pltpu.make_async_remote_copy(
        src_ref=src, dst_ref=dst, send_sem=send_sem, recv_sem=recv_sem,
        device_id=device, device_id_type=MESH,
    )


def signal(barrier, device):
    pl.semaphore_signal(barrier, inc=1, device_id=device, device_id_type=MESH)


def turn(value, step, size):
    return lax.rem(value + step + size, size)


def block(ref, number, rows):
    return ref.at[pl.ds(pl.multiple_of(number * rows, rows), rows)]


class Spread:
    def __init__(self, chunk, rows, cols, sems):
        self.chunk, self.rows, self.cols = chunk, rows, cols
        (self.zs, self.zr, self.fs, self.fr, self.ps, self.pr,
         self.xs, self.xr, self.cs, self.cr, self.own) = sems
        g, r, c = place()
        self.g, self.r, self.c = g, r, c
        self.x, self.yh, self.yl, self.z = r // 4, r % 4, c // 8, c % 8

    @staticmethod
    def semaphores():
        dma = pltpu.SemaphoreType.DMA
        return [dma((7,)), dma((7,)), dma((8,)), dma((8,)), dma((4,)), dma((4,)),
                dma((3,)), dma((3,)), dma((4,)), dma((4,)), dma((2,))]

    def target(self, j):
        return (self.r % 2, (self.c // 4) * 4 + j, self.g * 8 + self.r // 2)

    def source(self, i):
        return (self.c // 8, (2 * self.c + self.g) % 16, self.x * 4 + i)

    def is_me(self, device):
        return (device[0] == self.g) & (device[1] == self.r) & (device[2] == self.c)

    def greet(self, barrier):
        g, r, c = self.g, self.r, self.c
        for dz in range(1, 8):
            signal(barrier, (g, r, self.yl * 8 + turn(self.z, -dz, 8)))
        signal(barrier, (g, r, (1 - self.yl) * 8 + self.z))
        for dx in range(1, 4):
            signal(barrier, (g, turn(self.x, -dx, 4) * 4 + self.yh, c))
        signal(barrier, (1 - g, r, c))
        count = jnp.int32(12)
        for i in range(4):
            source = self.source(i)

            @pl.when(jnp.logical_not(self.is_me(source)))
            def _():
                signal(barrier, source)

            count += jnp.where(self.is_me(self.target(i)), 0, 1)
        return count

    def crossing(self, j):
        slot = (self.r % 2) * 16 + self.c
        return remote(self.chunk, block(self.cols, slot, CHUNK), self.ps.at[j],
                      self.pr.at[self.c % 4], self.target(j))

    def arriving(self, i):
        slot = self.g * 16 + self.x * 4 + i
        return remote(self.chunk, block(self.cols, slot, CHUNK), self.ps.at[i],
                      self.pr.at[i], self.source(i))

    def crossing_own(self):
        slot = (self.r % 2) * 16 + self.c
        return pltpu.make_async_copy(self.chunk, block(self.cols, slot, CHUNK), self.own.at[0])

    def across_z(self, dz, slot_z):
        return remote(self.chunk, block(self.rows, self.yl * 8 + slot_z, CHUNK),
                      self.zs.at[dz - 1], self.zr.at[dz - 1],
                      (self.g, self.r, self.yl * 8 + turn(self.z, dz, 8)))

    def partner(self, dz, side):
        slot = side * 8 + turn(self.z, -dz, 8)
        src = self.chunk if dz == 0 else block(self.rows, slot, CHUNK)
        return remote(src, block(self.rows, slot, CHUNK), self.fs.at[dz], self.fr.at[dz],
                      (self.g, self.r, (1 - self.yl) * 8 + self.z))

    def across_x(self, dx, x):
        part = block(self.cols, self.g * 4 + x, 4 * CHUNK)
        return remote(part, part, self.xs.at[dx - 1], self.xr.at[dx - 1],
                      (self.g, turn(self.x, dx, 4) * 4 + self.yh, self.c))

    def sibling(self, dx, grp):
        part = block(self.cols, grp * 4 + turn(self.x, -dx, 4), 4 * CHUNK)
        return remote(part, part, self.cs.at[dx], self.cr.at[dx], (1 - self.g, self.r, self.c))

    def own_row_copy(self):
        return pltpu.make_async_copy(self.chunk, block(self.rows, self.c, CHUNK), self.own.at[1])

    def begin(self):
        for j in range(4):
            me = self.is_me(self.target(j))

            @pl.when(me)
            def _():
                self.crossing_own().start()

            @pl.when(jnp.logical_not(me))
            def _():
                self.crossing(j).start()

        for dz in range(1, 8):
            self.across_z(dz, self.z).start()
        self.partner(0, self.yl).start()
        self.own_row_copy().start()

    def first_columns(self):
        for i in range(4):
            me = self.is_me(self.source(i))

            @pl.when(me)
            def _():
                self.crossing_own().wait()

            @pl.when(jnp.logical_not(me))
            def _():
                self.arriving(i).wait_recv()

        for dx in range(1, 4):
            self.across_x(dx, self.x).start()
        self.sibling(0, self.g).start()

    def pass_rows(self):
        for dz in range(1, 8):
            self.across_z(dz, turn(self.z, -dz, 8)).wait_recv()
            self.partner(dz, self.yl).start()

    def pass_columns(self):
        for dx in range(1, 4):
            self.across_x(dx, turn(self.x, -dx, 4)).wait_recv()
            self.sibling(dx, self.g).start()

    def finish(self):
        self.own_row_copy().wait()
        for dz in range(8):
            self.partner(dz, 1 - self.yl).wait_recv()
        for dx in range(4):
            self.sibling(dx, 1 - self.g).wait_recv()

    def drain(self):
        for j in range(4):
            @pl.when(jnp.logical_not(self.is_me(self.target(j))))
            def _():
                self.crossing(j).wait_send()

        for dz in range(1, 8):
            self.across_z(dz, self.z).wait_send()
        for dz in range(8):
            self.partner(dz, self.yl).wait_send()
        for dx in range(1, 4):
            self.across_x(dx, self.x).wait_send()
        for dx in range(4):
            self.sibling(dx, self.g).wait_send()


class Corner:
    def __init__(self, front, corner, sems):
        self.front, self.corner = front, corner
        self.ts, self.tr, self.ys, self.yr, self.xs, self.xr, self.cs, self.cr = sems
        self.g, self.r, self.c = place()
        self.x, self.yh = self.r // 4, self.r % 4
        self.q = self.g * 16 + self.r
        self.rows = corner.shape[0] // 32
        self.lanes = corner.shape[1]

    @staticmethod
    def semaphores():
        dma = pltpu.SemaphoreType.DMA
        return [dma((32,)), dma, dma((3,)), dma((3,)), dma((3,)), dma((3,)), dma((4,)), dma((4,))]

    def greet(self, barrier):
        @pl.when(self.c == 0)
        def _():
            for dy in range(1, 4):
                signal(barrier, (self.g, self.x * 4 + turn(self.yh, -dy, 4), self.c))

            @pl.when(self.q != 0)
            def _():
                signal(barrier, (0, 0, 0))

        return jnp.where(self.c == 0, 3, 0) + jnp.where((self.q == 0) & (self.c == 0), 31, 0)

    def piece(self, slot):
        start = pl.multiple_of(slot * self.rows, self.rows)
        return self.front.at[pl.ds(start, self.rows), pl.ds(0, self.lanes)]

    def handing(self, slot):
        return remote(self.piece(slot), block(self.corner, slot, self.rows), self.ts.at[slot],
                      self.tr, (slot // 16, slot % 16, 0))

    def keeping(self):
        return pltpu.make_async_copy(self.piece(0), block(self.corner, 0, self.rows), self.tr)

    def across_y(self, dy, yh):
        part = block(self.corner, self.g * 16 + self.x * 4 + yh, self.rows)
        return remote(part, part, self.ys.at[dy - 1], self.yr.at[dy - 1],
                      (self.g, self.x * 4 + turn(self.yh, dy, 4), self.c))

    def across_x(self, dx, x):
        part = block(self.corner, self.g * 4 + x, 4 * self.rows)
        return remote(part, part, self.xs.at[dx - 1], self.xr.at[dx - 1],
                      (self.g, turn(self.x, dx, 4) * 4 + self.yh, self.c))

    def sibling(self, dx, grp):
        part = block(self.corner, grp * 4 + turn(self.x, -dx, 4), 4 * self.rows)
        return remote(part, part, self.cs.at[dx], self.cr.at[dx], (1 - self.g, self.r, self.c))

    def begin(self):
        @pl.when((self.q == 0) & (self.c == 0))
        def _():
            self.keeping().start()

            @pl.loop(1, 32)
            def _(slot):
                self.handing(slot).start()

    def relay(self):
        @pl.when(self.c == 0)
        def _():
            @pl.when(self.q == 0)
            def _():
                self.keeping().wait()

            @pl.when(self.q != 0)
            def _():
                self.handing(self.q).wait_recv()

            for dy in range(1, 4):
                self.across_y(dy, self.yh).start()
            for dy in range(1, 4):
                self.across_y(dy, turn(self.yh, -dy, 4)).wait_recv()
            for dx in range(1, 4):
                self.across_x(dx, self.x).start()
            self.sibling(0, self.g).start()
            for dx in range(1, 4):
                self.across_x(dx, turn(self.x, -dx, 4)).wait_recv()
                self.sibling(dx, self.g).start()
            for dx in range(4):
                self.sibling(dx, 1 - self.g).wait_recv()

    def drain(self):
        @pl.when(self.c == 0)
        def _():
            @pl.when(self.q == 0)
            def _():
                @pl.loop(1, 32)
                def _(slot):
                    self.handing(slot).wait_send()

            for dy in range(1, 4):
                self.across_y(dy, self.yh).wait_send()
            for dx in range(1, 4):
                self.across_x(dx, self.x).wait_send()
            for dx in range(4):
                self.sibling(dx, self.g).wait_send()


def gather_kernel(chunk, front, rows, cols, corner, *sems):
    split = len(Spread.semaphores())
    spread = Spread(chunk, rows, cols, sems[:split])
    square = Corner(front, corner, sems[split:])
    barrier = pltpu.get_barrier_semaphore()
    count = spread.greet(barrier) + square.greet(barrier)
    pl.semaphore_wait(barrier, count)
    square.begin()
    spread.begin()
    spread.first_columns()
    spread.pass_rows()
    spread.pass_columns()
    square.relay()
    spread.finish()
    spread.drain()
    square.drain()


def share_kernel(left, right, pivots, chunk, second, shared, rows, cols, *sems):
    split = len(Spread.semaphores())
    spread = Spread(chunk, rows, cols, sems[:split])
    send, recv, own = sems[split:]
    g, r, c = place()
    barrier = pltpu.get_barrier_semaphore()
    count = spread.greet(barrier)

    @pl.when(c != 0)
    def _():
        signal(barrier, (g, r, 0))

    pl.semaphore_wait(barrier, count + jnp.where(c == 0, 15, 0))

    def handed(number, to):
        device = (g, r, to)
        if number == 0:
            return remote(block(left, to, CHUNK), chunk, send.at[0, to], recv.at[0], device)
        if number == 1:
            return remote(block(right, to, CHUNK), second, send.at[1, to], recv.at[1], device)
        return remote(pivots, shared, send.at[2, to], recv.at[2], device)

    kept = (
        pltpu.make_async_copy(block(left, 0, CHUNK), chunk, own.at[0]),
        pltpu.make_async_copy(block(right, 0, CHUNK), second, own.at[1]),
        pltpu.make_async_copy(pivots, shared, own.at[2]),
    )

    @pl.when(c == 0)
    def _():
        for number in range(3):
            for to in range(1, 16):
                handed(number, to).start()
            kept[number].start()
        kept[0].wait()

    @pl.when(c != 0)
    def _():
        handed(0, c).wait_recv()

    spread.begin()
    spread.first_columns()
    spread.pass_rows()
    spread.pass_columns()
    spread.finish()
    spread.drain()

    @pl.when(c == 0)
    def _():
        for number in range(3):
            for to in range(1, 16):
                handed(number, to).wait_send()
        kept[1].wait()
        kept[2].wait()

    @pl.when(c != 0)
    def _():
        handed(1, c).wait_recv()
        handed(2, c).wait_recv()


def times(a, b, dims, precision=None):
    return lax.dot_general(
        a, b, (dims, ((), ())), precision=precision, preferred_element_type=F32
    )


NN = ((1,), (0,))
NT = ((1,), (1,))
TN = ((0,), (0,))


def eliminate(work, inverse, pivots, recips, columns, small):
    def panel(first):
        def step(number, carry):
            top = pl.multiple_of(number * 8, 8)
            lane = [jnp.full((8, HALF), top + k, jnp.int32) for k in range(8)]
            head = work[pl.ds(top, 8), 0:HALF]
            for k in range(8):
                small[8 * k:8 * k + 8, :] = jnp.take_along_axis(head, lane[k], axis=1)
            for i in range(first, 16):
                tile = work[8 * i:8 * i + 8, 0:HALF]
                for k in range(8):
                    columns[8 * (8 * i + k):8 * (8 * i + k) + 8, :] = jnp.take_along_axis(
                        tile, lane[k], axis=1
                    )
            value = {}
            for k in range(8):
                for j in range(k, 8):
                    value[j, k] = jnp.broadcast_to(
                        small[8 * k + j:8 * k + j + 1, :], (8, HALF)
                    )
            small[64:72, :] = head
            small[72:80, :] = work[pl.ds(top, 8), HALF:2 * HALF]
            row = [
                [
                    jnp.broadcast_to(small[64 + 8 * part + k:65 + 8 * part + k, :], (8, HALF))
                    for part in range(2)
                ]
                for k in range(8)
            ]
            factor = {}
            recip = []
            for k in range(8):
                recip.append(1.0 / value[k, k])
                for j in range(k + 1, 8):
                    factor[j, k] = value[j, k] * recip[k]
                for j in range(k + 1, 8):
                    for i in range(j, 8):
                        value[i, j] = value[i, j] - factor[j, k] * value[i, k]
                    for part in range(2):
                        row[j][part] = row[j][part] - factor[j, k] * row[k][part]
            ids = lax.broadcasted_iota(jnp.int32, (8, HALF), 0)
            kept = [row[0][1], value[0, 0], recip[0]]
            for k in range(1, 8):
                kept[0] = jnp.where(ids == k, row[k][1], kept[0])
                kept[1] = jnp.where(ids == k, value[k, k], kept[1])
                kept[2] = jnp.where(ids == k, recip[k], kept[2])
            inverse[pl.ds(top, 8), :] = kept[0]
            pivots[pl.ds(top, 8), :] = kept[1]
            recips[pl.ds(top, 8), :] = kept[2]
            for k in range(7, -1, -1):
                for part in range(2):
                    total = row[k][part] * recip[k]
                    for j in range(k + 1, 8):
                        total = total - factor[j, k] * row[j][part]
                    row[k][part] = total
            for i in range(first, 16):
                for part in range(2):
                    at = (slice(8 * i, 8 * i + 8), slice(part * HALF, (part + 1) * HALF))
                    total = work[at]
                    for k in range(8):
                        total = total - (
                            columns[8 * (8 * i + k):8 * (8 * i + k) + 8, :] * row[k][part]
                        )
                    work[at] = total
            return carry

        return step

    for quarter in range(4):
        lax.fori_loop(quarter * 4, quarter * 4 + 4, panel(quarter * 4), 0)


def factor(square, order, work, inverse, pivots, recips, columns, small):
    size = square.shape[0]
    ids = lax.broadcasted_iota(jnp.int32, (size, size), 0)
    chosen = (ids == order).astype(F32)
    moved = times(chosen, times(square, chosen, NN, EXACT), TN, EXACT)
    eye = (
        lax.broadcasted_iota(jnp.int32, (HALF, HALF), 0)
        == lax.broadcasted_iota(jnp.int32, (HALF, HALF), 1)
    ).astype(F32)
    lo, hi = slice(0, HALF), slice(HALF, 2 * HALF)
    work[:, lo] = moved[lo, lo]
    work[:, hi] = eye
    eliminate(work, inverse.at[lo], pivots.at[lo], recips.at[lo], columns, small)
    first = inverse[lo, :]
    upper = times(first, moved[lo, hi], NN, EXACT)
    scaled = upper * recips[lo, :]
    work[:, lo] = moved[hi, hi] - times(scaled, upper, TN, EXACT)
    work[:, hi] = eye
    below = times(scaled, first, TN, EXACT)
    eliminate(work, inverse.at[hi], pivots.at[hi], recips.at[hi], columns, small)
    second = inverse[hi, :]
    cross = -times(second, below, NN, EXACT)
    top = jnp.concatenate([first * recips[lo, :], jnp.zeros((HALF, HALF), F32)], axis=1)
    low = jnp.concatenate([cross * recips[hi, :], second * recips[hi, :]], axis=1)
    solver = times(jnp.concatenate([top, low], axis=0), chosen, NT, EXACT)
    values = jnp.concatenate([pivots[lo, :].T[0:1, :], pivots[hi, :].T[0:1, :]], axis=1)
    return solver, values


def panels_kernel(whole, rows, cols, corner, prev_pivots, orders, left, right, pivot_rows, front, landed, *scratch):
    g, r, c = place()

    @pl.when(c == 0)
    def _():
        lo, hi = slice(0, WIDTH), slice(WIDTH, 2 * WIDTH)
        fetch = pltpu.make_async_copy(whole.at[:, 0:2 * WIDTH], front, landed)
        fetch.start()
        near = cols[0:2 * WIDTH, :]
        before = prev_pivots[...]
        near_scaled = (near.astype(F32) * before).astype(BF16)
        rows_scaled = (rows[...].astype(F32) * before).astype(BF16)
        both = times(near_scaled[lo], near[lo], NT) + times(near[lo], near_scaled[lo], NT)
        solver, values = factor(corner[lo, lo] - 0.5 * both, orders[0:1, :], *scratch)
        pivot_rows[0:1, :] = values
        fetch.wait()
        panel = front[:, lo] - times(rows_scaled, near[lo], NT)
        shown = times(panel, solver, NT, EXACT).astype(BF16)
        left[...] = shown
        edge = corner[hi, lo] - times(near_scaled[hi], near[lo], NT)
        edge = times(edge, solver, NT, EXACT).astype(BF16)
        edge_scaled = (edge.astype(F32) * values).astype(BF16)
        both = times(near_scaled[hi], near[hi], NT) + times(near[hi], near_scaled[hi], NT)
        more = times(edge_scaled, edge, NT) + times(edge, edge_scaled, NT)
        square = (corner[hi, hi] - 0.5 * both) - 0.5 * more
        solver, later = factor(square, orders[1:2, :], *scratch)
        pivot_rows[1:2, :] = later
        shown_scaled = (shown.astype(F32) * values).astype(BF16)
        panel = front[:, hi] - times(rows_scaled, near[hi], NT)
        panel = panel - times(shown_scaled, edge, NT)
        right[...] = times(panel, solver, NT, EXACT).astype(BF16)


def body(front, prev_lower, prev_pivots, pivot_order):
    row_count, col_count = front.shape
    width = prev_lower.shape[1]
    g, r, c = place()
    vmem = pl.BlockSpec(memory_space=pltpu.VMEM)
    shape = jax.ShapeDtypeStruct
    dma = pltpu.SemaphoreType.DMA
    rows, cols, corner = pl.pallas_call(
        gather_kernel,
        out_shape=[
            shape((row_count, width), BF16),
            shape((col_count, width), BF16),
            shape((2 * width, 2 * width), F32),
        ],
        in_specs=[vmem, pl.BlockSpec(memory_space=pl.ANY)],
        out_specs=[vmem] * 3,
        scratch_shapes=Spread.semaphores() + Corner.semaphores(),
        compiler_params=pltpu.CompilerParams(
            collective_id=0, has_side_effects=True, vmem_limit_bytes=VMEM_LIMIT
        ),
        name="gather",
    )(prev_lower, front)
    left, right, pivot_rows = pl.pallas_call(
        panels_kernel,
        out_shape=[
            shape((row_count, width), BF16),
            shape((row_count, width), BF16),
            shape((2, width), F32),
        ],
        in_specs=[pl.BlockSpec(memory_space=pl.ANY)] + [vmem] * 5,
        out_specs=[vmem] * 3,
        scratch_shapes=[
            pltpu.VMEM((row_count, 2 * width), F32),
            dma,
            pltpu.VMEM((HALF, 2 * HALF), F32),
            pltpu.VMEM((2 * HALF, HALF), F32),
            pltpu.VMEM((2 * HALF, HALF), F32),
            pltpu.VMEM((2 * HALF, HALF), F32),
            pltpu.VMEM((8 * HALF, HALF), F32),
            pltpu.VMEM((80, HALF), F32),
        ],
        compiler_params=pltpu.CompilerParams(vmem_limit_bytes=VMEM_LIMIT),
        name="panels",
    )(front, rows, cols, corner, prev_pivots.reshape(1, width), pivot_order)
    chunk, second, shared, new_rows, new_cols = pl.pallas_call(
        share_kernel,
        out_shape=[
            shape((CHUNK, width), BF16),
            shape((CHUNK, width), BF16),
            shape((2, width), F32),
            shape((row_count, width), BF16),
            shape((col_count, width), BF16),
        ],
        in_specs=[vmem] * 3,
        out_specs=[vmem] * 5,
        scratch_shapes=Spread.semaphores() + [dma((3, 16)), dma((3,)), dma((3,))],
        compiler_params=pltpu.CompilerParams(
            collective_id=1, has_side_effects=True, vmem_limit_bytes=VMEM_LIMIT
        ),
        name="share",
    )(left, right, pivot_rows)

    first_row = (g * 16 + r) * row_count
    row_ids = first_row + lax.broadcasted_iota(jnp.int32, (row_count, 1), 0)
    col_ids = c * col_count + lax.broadcasted_iota(jnp.int32, (col_count, 1), 0)
    own_ids = first_row + c * CHUNK + lax.broadcasted_iota(jnp.int32, (CHUNK, 1), 0)
    none = jnp.zeros((), BF16)
    new_rows = jnp.where(row_ids >= width, new_rows, none)
    new_cols = jnp.where(col_ids >= width, new_cols, none)
    second = jnp.where(own_ids >= width, second, none)
    scaled = jnp.concatenate(
        [
            (rows.astype(F32) * prev_pivots).astype(BF16),
            (new_rows.astype(F32) * shared[0]).astype(BF16),
        ],
        axis=1,
    )
    schur = front - times(scaled, jnp.concatenate([cols, new_cols], axis=1), NT)
    panels = jnp.concatenate([chunk.astype(F32) * shared[0], second.astype(F32) * shared[1]], axis=1)
    return schur, panels, shared.reshape(2 * width)


def solution(mesh):
    in_specs = (P(("grp", "row"), "col"), P(("grp", "row", "col"), None), P(), P())
    out_specs = (P(("grp", "row"), "col"), P(("grp", "row", "col"), None), P())
    return jax.shard_map(body, mesh=mesh, in_specs=in_specs, out_specs=out_specs, check_vma=False)
```

time: 1040 us -> 107 us (0.10); the launches traced: 1030 us -> 107 us
  waiting for transfers between devices: 840 us -> 0 us
  other arithmetic: 114 us -> 3.13 us
  Pallas kernels: 0 us -> 99.8 us
  blocking collectives: 20.2 us -> 0 us
  local copies, waits for them, and re-layouts: 20.7 us -> 1.37 us
  between operations: 17.1 us -> 0.77 us
  matrix products: 15.4 us -> 2.08 us
    psum x2 -> x0, waiting for transfers between devices: 550 us -> none  [spread(): return lax.psum(jnp.where(mine, array, jnp.zeros_like(array)), axis)]
    all_gather x4 -> x0, waiting for transfers between devices: 290 us -> none  [picked(): lax.all_gather(array, axis)]
    another operation x18 -> x0, other arithmetic: 108 us -> none  [the longest x13 68.5 us: factor_panel(): cholesky_factor = jnp.linalg.cholesky(permuted)]
    pallas_call x0 -> x3, Pallas kernels: none -> 99.8 us  [the longest x1 44.7 us: body(): pl.pallas_call(gather_kernel, out_shape=[shape((row_count, width), BF16),...]
    all_to_all x1 -> x0, blocking collectives: 20.2 us -> none  [copy_for_each(): return lax.all_to_all(copies, axis, split_axis=0, concat_axis=0, tiled=True)]
  transfers between devices with their start and end apart: 6 -> 0, of which waited for: 6 -> 0; matrix products, arithmetic and copies ran while one was open for 1% -> 0% of each run, Pallas kernels for 0% -> 0%
where the time goes in v1:
time: 107 us
  Pallas kernels  99.8 us (93%)
  other arithmetic  3.13 us (3%)
  matrix products  2.08 us (2%)
  local copies, waits for them, and re-layouts  1.37 us (1%)
    pallas_call x1, Pallas kernels, body(): pl.pallas_call(gather_kernel, out_shape=[shape((row_count, width), BF16),...  44.7 us
    pallas_call x1, Pallas kernels, body(): pl.pallas_call(panels_kernel, out_shape=[shape((row_count, width), BF16),...  29.7 us
    pallas_call x1, Pallas kernels, body(): pl.pallas_call(share_kernel, out_shape=[shape((CHUNK, width), BF16), shap...  25.4 us

profile of v1, /device:TPU:1, one launch (start us, length us, event | category | flops | bytes accessed | tf_op | source)
XLA Modules:
  0.0 107.1 jit_solution(14861543861390302556)
XLA Ops:
  0.6 44.7 %gather.1 = (bf16[512,256]{1,0:T(8,128)(2,1)}, bf16[1024,256]{1,0:T(8,128)(2,1)}, f32[512,512]{1,0:T(8,128)}) custom-call(bf16[32,256]{1,0:T(8,128)(2,1)} %chunk.1, f32[512,1024]{1,0:T(8,128)} %whole.1), custom_call_target="tpu_custom_call" | custom-call | tf_op jit(solution)/shard_map/gather/pallas_call | solution.py:520
  45.3 0.0 copy-start.2
  45.3 0.0 copy-start.6
  45.3 29.7 %panels.1 = (bf16[512,256]{1,0:T(8,128)(2,1)}, bf16[512,256]{1,0:T(8,128)(2,1)}, f32[2,256]{1,0:T(2,128)}) custom-call(f32[512,1024]{1,0:T(8,128)} %whole.1, bf16[512,256]{1,0:T(8,128)(2,1)} %get-tuple-element.14.rows, bf16[1024,256]{1,0:T(8,128)(2,1)} %get-tuple-element.15.cols, f32[512,512]{1,0:T(8,128)} %get-tuple-element.16.corner, f32[1,256]{1,0:T(1,128)} %bitcast.9, ...), custom_call_target="tpu_custom_call" | custom-call | tf_op jit(solution)/shard_map/panels/pallas_call | solution.py:535
  75.0 0.0 copy-start
  75.1 0.0 copy-start.1
  75.1 25.4 %share.1 = (bf16[32,256]{1,0:T(8,128)(2,1)}, bf16[32,256]{1,0:T(8,128)(2,1)}, f32[2,256]{1,0:T(2,128)}, bf16[512,256]{1,0:T(8,128)(2,1)}, bf16[1024,256]{1,0:T(8,128)(2,1)}) custom-call(bf16[512,256]{1,0:T(8,128)(2,1)} %get-tuple-element.17.left, bf16[512,256]{1,0:T(8,128)(2,1)} %get-tuple-element.18.right, f32[2,256]{1,0:T(2,128)} %get-tuple-element.19.pivots), custom_call_target="tpu_custom_call" | custom-call | tf_op jit(solution)/shard_map/share/pallas_call | solution.py:557
  100.5 1.2 %broadcast_select_fusion = bf16[1024,256]{1,0:T(8,128)(2,1)S(1)} fusion(bf16[1024,256]{1,0:T(8,128)(2,1)} %get-tuple-element.22, pred[1024]{0:T(1024)(128)(4,1)S(1)} %add_compare_fusion), kind=kLoop, calls=%fused_computation.9 | loop fusion | flops 262144 | bytes 1049600 | tf_op jit(solution)/shard_map/jit(_where)/select_n | solution.py:581
  101.7 0.8 fusion.7
  102.5 0.0 copy-done.2
  102.5 0.0 copy-done.6
  102.5 1.2 %multiply_convert_fusion = (bf16[512,256]{1,0:T(8,128)(2,1)S(1)}, bf16[512,256]{1,0:T(8,128)(2,1)S(1)}) fusion(f32[256]{0:T(256)S(1)} %bitcast.5, bf16[512,256]{1,0:T(8,128)(2,1)} %get-tuple-element.20, pred[512]{0:T(512)(128)(4,1)S(1)} %add_compare_fusion.1, f32[256]{0:T(256)S(1)} %copy-done.6, bf16[512,256]{1,0:T(8,128)(2,1)S(1)} %copy-done.2), kind=kLoop, calls=%fused_computation.7 | loop fusion | flops 917504 | bytes 1051136 | tf_op jit(solution)/shard_map/convert_element_type | solution.py:586
  103.7 0.0 copy-done
  103.7 0.0 copy-done.1
  103.7 0.0 copy-start.3
  103.7 0.0 copy-start.4
  103.7 0.0 copy-start.5
  103.7 2.1 %convolution_subtract_fusion = f32[512,1024]{1,0:T(8,128)} fusion(f32[512,1024]{1,0:T(8,128)S(1)} %copy-done, bf16[1024,256]{1,0:T(8,128)(2,1)S(1)} %broadcast_select_fusion, bf16[1024,256]{1,0:T(8,128)(2,1)S(1)} %copy-done.1, bf16[512,256]{1,0:T(8,128)(2,1)S(1)} %get-tuple-element.29, bf16[512,256]{1,0:T(8,128)(2,1)S(1)} %get-tuple-element.30), kind=kOutput, calls=%fused_computation | convolution fusion | flops 540540928 | bytes 5767168 | tf_op jit(solution)/shard_map/dot_general | solution.py:369
  105.8 0.0 copy-done.3
  105.8 0.0 copy-done.4
  105.8 0.1 convert_multiply_fusion
  105.9 0.6 pad_maximum_fusion
  106.5 0.0 copy-done.5
  106.6 0.6 copy.7
  (3 shorter events, 0.0 us)
Async XLA Ops:
  45.3 57.2 %copy-start.2 = (bf16[512,256]{1,0:T(8,128)(2,1)S(1)}, bf16[512,256]{1,0:T(8,128)(2,1)}, u32[]{:S(2)}) copy-start(bf16[512,256]{1,0:T(8,128)(2,1)} %get-tuple-element.14.rows) | copy-start | bytes 786436
  45.3 57.2 %copy-start.6 = (f32[256]{0:T(256)S(1)}, f32[256]{0:T(256)}, u32[]{:S(2)}) copy-start(f32[256]{0:T(256)} %param.6) | copy-start | bytes 3076
  75.0 28.6 %copy-start = (f32[512,1024]{1,0:T(8,128)S(1)}, f32[512,1024]{1,0:T(8,128)}, u32[]{:S(2)}) copy-start(f32[512,1024]{1,0:T(8,128)} %whole.1) | copy-start | bytes 6291460
  75.1 28.6 %copy-start.1 = (bf16[1024,256]{1,0:T(8,128)(2,1)S(1)}, bf16[1024,256]{1,0:T(8,128)(2,1)}, u32[]{:S(2)}) copy-start(bf16[1024,256]{1,0:T(8,128)(2,1)} %get-tuple-element.15.cols) | copy-start | bytes 1572868
  103.7 2.1 %copy-start.3 = (bf16[32,256]{1,0:T(8,128)(2,1)S(1)}, bf16[32,256]{1,0:T(8,128)(2,1)}, u32[]{:S(2)}) copy-start(bf16[32,256]{1,0:T(8,128)(2,1)} %get-tuple-element.23) | copy-start | bytes 49156
  103.7 2.1 %copy-start.4 = (bf16[32,256]{1,0:T(8,128)(2,1)S(1)}, bf16[32,256]{1,0:T(8,128)(2,1)}, u32[]{:S(2)}) copy-start(bf16[32,256]{1,0:T(8,128)(2,1)} %get-tuple-element.24) | copy-start | bytes 49156
  103.7 2.8 %copy-start.5 = (f32[2,256]{1,0:T(2,128)S(1)}, f32[2,256]{1,0:T(2,128)}, u32[]{:S(2)}) copy-start(f32[2,256]{1,0:T(2,128)} %get-tuple-element.21) | copy-start | bytes 6148

commit v2 on v1

--- a/solution.py
+++ b/solution.py
@@ -39,8 +39,8 @@
 
 
 class Spread:
-    def __init__(self, chunk, rows, cols, sems):
-        self.chunk, self.rows, self.cols = chunk, rows, cols
+    def __init__(self, chunk, rows, cols, sems, full=None):
+        self.chunk, self.rows, self.cols, self.full = chunk, rows, cols, full
         (self.zs, self.zr, self.fs, self.fr, self.ps, self.pr,
          self.xs, self.xr, self.cs, self.cr, self.own) = sems
         g, r, c = place()
@@ -102,7 +102,8 @@
 
     def partner(self, dz, side):
         slot = side * 8 + turn(self.z, -dz, 8)
-        src = self.chunk if dz == 0 else block(self.rows, slot, CHUNK)
+        held = self.rows if self.full is None else self.full
+        src = self.chunk if dz == 0 else block(held, slot, CHUNK)
         return remote(src, block(self.rows, slot, CHUNK), self.fs.at[dz], self.fr.at[dz],
                       (self.g, self.r, (1 - self.yl) * 8 + self.z))
 
@@ -132,7 +133,8 @@
 
         for dz in range(1, 8):
             self.across_z(dz, self.z).start()
-        self.partner(0, self.yl).start()
+        for dz in range(1 if self.full is None else 8):
+            self.partner(dz, self.yl).start()
         self.own_row_copy().start()
 
     def first_columns(self):
@@ -154,7 +156,8 @@
     def pass_rows(self):
         for dz in range(1, 8):
             self.across_z(dz, turn(self.z, -dz, 8)).wait_recv()
-            self.partner(dz, self.yl).start()
+            if self.full is None:
+                self.partner(dz, self.yl).start()
 
     def pass_columns(self):
         for dx in range(1, 4):
@@ -185,8 +188,8 @@
 
 
 class Corner:
-    def __init__(self, front, corner, sems):
-        self.front, self.corner = front, corner
+    def __init__(self, front, first, corner, sems):
+        self.front, self.first, self.corner = front, first, corner
         self.ts, self.tr, self.ys, self.yr, self.xs, self.xr, self.cs, self.cr = sems
         self.g, self.r, self.c = place()
         self.x, self.yh = self.r // 4, self.r % 4
@@ -212,7 +215,7 @@
         return jnp.where(self.c == 0, 3, 0) + jnp.where((self.q == 0) & (self.c == 0), 31, 0)
 
     def piece(self, slot):
-        start = pl.multiple_of(slot * self.rows, self.rows)
+        start = pl.multiple_of(self.first + slot * self.rows, self.rows)
         return self.front.at[pl.ds(start, self.rows), pl.ds(0, self.lanes)]
 
     def handing(self, slot):
@@ -245,124 +248,47 @@
             def _(slot):
                 self.handing(slot).start()
 
-    def relay(self):
-        @pl.when(self.c == 0)
+    def first_hop(self):
+        @pl.when(self.q == 0)
         def _():
-            @pl.when(self.q == 0)
-            def _():
-                self.keeping().wait()
-
-            @pl.when(self.q != 0)
-            def _():
-                self.handing(self.q).wait_recv()
-
-            for dy in range(1, 4):
-                self.across_y(dy, self.yh).start()
-            for dy in range(1, 4):
-                self.across_y(dy, turn(self.yh, -dy, 4)).wait_recv()
-            for dx in range(1, 4):
-                self.across_x(dx, self.x).start()
-            self.sibling(0, self.g).start()
-            for dx in range(1, 4):
-                self.across_x(dx, turn(self.x, -dx, 4)).wait_recv()
-                self.sibling(dx, self.g).start()
-            for dx in range(4):
-                self.sibling(dx, 1 - self.g).wait_recv()
+            self.keeping().wait()
+
+        @pl.when(self.q != 0)
+        def _():
+            self.handing(self.q).wait_recv()
+
+        for dy in range(1, 4):
+            self.across_y(dy, self.yh).start()
+
+    def second_hop(self):
+        for dy in range(1, 4):
+            self.across_y(dy, turn(self.yh, -dy, 4)).wait_recv()
+        for dx in range(1, 4):
+            self.across_x(dx, self.x).start()
+        self.sibling(0, self.g).start()
+
+    def third_hop(self):
+        for dx in range(1, 4):
+            self.across_x(dx, turn(self.x, -dx, 4)).wait_recv()
+            self.sibling(dx, self.g).start()
+
+    def finish(self):
+        for dx in range(4):
+            self.sibling(dx, 1 - self.g).wait_recv()
 
     def drain(self):
-        @pl.when(self.c == 0)
+        @pl.when(self.q == 0)
         def _():
-            @pl.when(self.q == 0)
-            def _():
-                @pl.loop(1, 32)
-                def _(slot):
-                    self.handing(slot).wait_send()
-
-            for dy in range(1, 4):
-                self.across_y(dy, self.yh).wait_send()
-            for dx in range(1, 4):
-                self.across_x(dx, self.x).wait_send()
-            for dx in range(4):
-                self.sibling(dx, self.g).wait_send()
-
-
-def gather_kernel(chunk, front, rows, cols, corner, *sems):
-    split = len(Spread.semaphores())
-    spread = Spread(chunk, rows, cols, sems[:split])
-    square = Corner(front, corner, sems[split:])
-    barrier = pltpu.get_barrier_semaphore()
-    count = spread.greet(barrier) + square.greet(barrier)
-    pl.semaphore_wait(barrier, count)
-    square.begin()
-    spread.begin()
-    spread.first_columns()
-    spread.pass_rows()
-    spread.pass_columns()
-    square.relay()
-    spread.finish()
-    spread.drain()
-    square.drain()
-
-
-def share_kernel(left, right, pivots, chunk, second, shared, rows, cols, *sems):
-    split = len(Spread.semaphores())
-    spread = Spread(chunk, rows, cols, sems[:split])
-    send, recv, own = sems[split:]
-    g, r, c = place()
-    barrier = pltpu.get_barrier_semaphore()
-    count = spread.greet(barrier)
-
-    @pl.when(c != 0)
-    def _():
-        signal(barrier, (g, r, 0))
-
-    pl.semaphore_wait(barrier, count + jnp.where(c == 0, 15, 0))
-
-    def handed(number, to):
-        device = (g, r, to)
-        if number == 0:
-            return remote(block(left, to, CHUNK), chunk, send.at[0, to], recv.at[0], device)
-        if number == 1:
-            return remote(block(right, to, CHUNK), second, send.at[1, to], recv.at[1], device)
-        return remote(pivots, shared, send.at[2, to], recv.at[2], device)
-
-    kept = (
-        pltpu.make_async_copy(block(left, 0, CHUNK), chunk, own.at[0]),
-        pltpu.make_async_copy(block(right, 0, CHUNK), second, own.at[1]),
-        pltpu.make_async_copy(pivots, shared, own.at[2]),
-    )
-
-    @pl.when(c == 0)
-    def _():
-        for number in range(3):
-            for to in range(1, 16):
-                handed(number, to).start()
-            kept[number].start()
-        kept[0].wait()
-
-    @pl.when(c != 0)
-    def _():
-        handed(0, c).wait_recv()
-
-    spread.begin()
-    spread.first_columns()
-    spread.pass_rows()
-    spread.pass_columns()
-    spread.finish()
-    spread.drain()
-
-    @pl.when(c == 0)
-    def _():
-        for number in range(3):
-            for to in range(1, 16):
-                handed(number, to).wait_send()
-        kept[1].wait()
-        kept[2].wait()
-
-    @pl.when(c != 0)
-    def _():
-        handed(1, c).wait_recv()
-        handed(2, c).wait_recv()
+            @pl.loop(1, 32)
+            def _(slot):
+                self.handing(slot).wait_send()
+
+        for dy in range(1, 4):
+            self.across_y(dy, self.yh).wait_send()
+        for dx in range(1, 4):
+            self.across_x(dx, self.x).wait_send()
+        for dx in range(4):
+            self.sibling(dx, self.g).wait_send()
 
 
 def times(a, b, dims, precision=None):
@@ -448,7 +374,7 @@
         lax.fori_loop(quarter * 4, quarter * 4 + 4, panel(quarter * 4), 0)
 
 
-def factor(square, order, work, inverse, pivots, recips, columns, small):
+def factor(square, order, halfway, work, inverse, pivots, recips, columns, small):
     size = square.shape[0]
     ids = lax.broadcasted_iota(jnp.int32, (size, size), 0)
     chosen = (ids == order).astype(F32)
@@ -461,6 +387,7 @@
     work[:, lo] = moved[lo, lo]
     work[:, hi] = eye
     eliminate(work, inverse.at[lo], pivots.at[lo], recips.at[lo], columns, small)
+    halfway()
     first = inverse[lo, :]
     upper = times(first, moved[lo, hi], NN, EXACT)
     scaled = upper * recips[lo, :]
@@ -477,71 +404,180 @@
     return solver, values
 
 
-def panels_kernel(whole, rows, cols, corner, prev_pivots, orders, left, right, pivot_rows, front, landed, *scratch):
+def window_kernel(
+    prev_chunk, whole, prev_pivots, orders,
+    left_side, right_side, panels, pivots_out,
+    rows, cols, new_rows, new_cols, chunk, second, shared,
+    left, right, values, corner, edges, front, landed,
+    work, inverse, pivots, recips, columns, small,
+    send, recv, *sems,
+):
     g, r, c = place()
+    q = g * 16 + r
+    split = len(Spread.semaphores())
+    deal = len(Corner.semaphores())
+    old = Spread(prev_chunk, rows, cols, sems[:split])
+    top_square = Corner(whole, 0, corner, sems[2 * split:2 * split + deal])
+    low_square = Corner(whole, WIDTH, edges, sems[2 * split + deal:])
+    scratch = (work, inverse, pivots, recips, columns, small)
+    lo, hi = slice(0, WIDTH), slice(WIDTH, 2 * WIDTH)
+
+    def handed(number, panel, to):
+        device = (g, r, to)
+        if number == 0:
+            source, landing = block((left, right)[panel], to, CHUNK), (chunk, second)[panel]
+        else:
+            source, landing = values.at[panel], shared.at[panel]
+        return remote(source, landing, send.at[2 * number + panel, to],
+                      recv.at[2 * number + panel], device)
+
+    barrier = pltpu.get_barrier_semaphore()
+    count = old.greet(barrier) + top_square.greet(barrier)
+
+    @pl.when(c != 0)
+    def _():
+        signal(barrier, (g, r, 0))
+
+    pl.semaphore_wait(barrier, count + jnp.where(c == 0, 15, 0))
+    top_square.begin()
+    old.begin()
+    low_square.begin()
+    fetch = pltpu.make_async_copy(whole.at[:, 0:2 * WIDTH], front, landed)
 
     @pl.when(c == 0)
     def _():
-        lo, hi = slice(0, WIDTH), slice(WIDTH, 2 * WIDTH)
-        fetch = pltpu.make_async_copy(whole.at[:, 0:2 * WIDTH], front, landed)
         fetch.start()
+        top_square.first_hop()
+
+    old.pass_rows()
+    old.first_columns()
+
+    @pl.when(c == 0)
+    def _():
+        top_square.second_hop()
+
+    old.pass_columns()
+
+    @pl.when(c == 0)
+    def _():
+        top_square.third_hop()
+        low_square.first_hop()
+
+    old.finish()
+    before = prev_pivots[...]
+    rows_scaled = (rows[...].astype(F32) * before).astype(BF16)
+    left_side[:, lo] = rows_scaled
+    right_side[:, lo] = cols[...]
+
+    @pl.when(c == 0)
+    def _():
+        new = Spread(block(left, 0, CHUNK), new_rows, new_cols, sems[split:2 * split], left)
         near = cols[0:2 * WIDTH, :]
-        before = prev_pivots[...]
         near_scaled = (near.astype(F32) * before).astype(BF16)
-        rows_scaled = (rows[...].astype(F32) * before).astype(BF16)
         both = times(near_scaled[lo], near[lo], NT) + times(near[lo], near_scaled[lo], NT)
-        solver, values = factor(corner[lo, lo] - 0.5 * both, orders[0:1, :], *scratch)
-        pivot_rows[0:1, :] = values
+        top_square.finish()
+        solver, given = factor(
+            corner[...] - 0.5 * both, orders[0:1, :], low_square.second_hop, *scratch
+        )
+        values[0] = jnp.broadcast_to(given, (8, WIDTH))
         fetch.wait()
-        panel = front[:, lo] - times(rows_scaled, near[lo], NT)
+        panel = front[:, lo] - times(left_side[:, lo], near[lo], NT)
         shown = times(panel, solver, NT, EXACT).astype(BF16)
         left[...] = shown
-        edge = corner[hi, lo] - times(near_scaled[hi], near[lo], NT)
+        low_square.third_hop()
+        low_square.finish()
+        edge = edges[:, lo] - times(near_scaled[hi], near[lo], NT)
         edge = times(edge, solver, NT, EXACT).astype(BF16)
-        edge_scaled = (edge.astype(F32) * values).astype(BF16)
+        for to in range(1, 16):
+            handed(0, 0, to).start()
+        new.begin()
+        for to in range(1, 16):
+            handed(1, 0, to).start()
+        chunk[...] = left[0:CHUNK, :]
+        edge_scaled = (edge.astype(F32) * given).astype(BF16)
         both = times(near_scaled[hi], near[hi], NT) + times(near[hi], near_scaled[hi], NT)
         more = times(edge_scaled, edge, NT) + times(edge, edge_scaled, NT)
-        square = (corner[hi, hi] - 0.5 * both) - 0.5 * more
-        solver, later = factor(square, orders[1:2, :], *scratch)
-        pivot_rows[1:2, :] = later
-        shown_scaled = (shown.astype(F32) * values).astype(BF16)
-        panel = front[:, hi] - times(rows_scaled, near[hi], NT)
+        square = (edges[:, hi] - 0.5 * both) - 0.5 * more
+        solver, later = factor(square, orders[1:2, :], lambda: None, *scratch)
+        values[1] = jnp.broadcast_to(later, (8, WIDTH))
+        shown_scaled = (left[...].astype(F32) * given).astype(BF16)
+        panel = front[:, hi] - times(left_side[:, lo], near[hi], NT)
         panel = panel - times(shown_scaled, edge, NT)
         right[...] = times(panel, solver, NT, EXACT).astype(BF16)
+        new.first_columns()
+        for to in range(1, 16):
+            handed(1, 1, to).start()
+            handed(0, 1, to).start()
+        second[...] = right[0:CHUNK, :]
+        shared[...] = values[...]
+        new.pass_rows()
+        new.pass_columns()
+        new.finish()
+        new.drain()
+        for to in range(1, 16):
+            for panel in range(2):
+                handed(0, panel, to).wait_send()
+                handed(1, panel, to).wait_send()
+        top_square.drain()
+        low_square.drain()
+
+    @pl.when(c != 0)
+    def _():
+        new = Spread(chunk, new_rows, new_cols, sems[split:2 * split])
+        handed(0, 0, c).wait_recv()
+        new.begin()
+        new.pass_rows()
+        new.first_columns()
+        new.pass_columns()
+        handed(1, 0, c).wait_recv()
+        handed(1, 1, c).wait_recv()
+        handed(0, 1, c).wait_recv()
+        new.finish()
+        new.drain()
+
+    old.drain()
+    row_ids = q * rows.shape[0] + lax.broadcasted_iota(jnp.int32, (rows.shape[0], 1), 0)
+    col_ids = c * cols.shape[0] + lax.broadcasted_iota(jnp.int32, (cols.shape[0], 1), 0)
+    own_ids = q * rows.shape[0] + c * CHUNK + lax.broadcasted_iota(jnp.int32, (CHUNK, 1), 0)
+    given, later = shared[0, 0:1, :], shared[1, 0:1, :]
+    live = jnp.where(row_ids >= WIDTH, new_rows[...].astype(F32), 0.0)
+    left_side[:, hi] = (live * given).astype(BF16)
+    right_side[:, hi] = jnp.where(col_ids >= WIDTH, new_cols[...].astype(F32), 0.0).astype(BF16)
+    panels[:, lo] = chunk[...].astype(F32) * given
+    panels[:, hi] = jnp.where(own_ids >= WIDTH, second[...].astype(F32), 0.0) * later
+    pivots_out[0:1, :] = given
+    pivots_out[1:2, :] = later
 
 
 def body(front, prev_lower, prev_pivots, pivot_order):
     row_count, col_count = front.shape
     width = prev_lower.shape[1]
-    g, r, c = place()
     vmem = pl.BlockSpec(memory_space=pltpu.VMEM)
     shape = jax.ShapeDtypeStruct
     dma = pltpu.SemaphoreType.DMA
-    rows, cols, corner = pl.pallas_call(
-        gather_kernel,
+    left_side, right_side, panels, pivots = pl.pallas_call(
+        window_kernel,
         out_shape=[
-            shape((row_count, width), BF16),
-            shape((col_count, width), BF16),
-            shape((2 * width, 2 * width), F32),
-        ],
-        in_specs=[vmem, pl.BlockSpec(memory_space=pl.ANY)],
-        out_specs=[vmem] * 3,
-        scratch_shapes=Spread.semaphores() + Corner.semaphores(),
-        compiler_params=pltpu.CompilerParams(
-            collective_id=0, has_side_effects=True, vmem_limit_bytes=VMEM_LIMIT
-        ),
-        name="gather",
-    )(prev_lower, front)
-    left, right, pivot_rows = pl.pallas_call(
-        panels_kernel,
-        out_shape=[
-            shape((row_count, width), BF16),
-            shape((row_count, width), BF16),
+            shape((row_count, 2 * width), BF16),
+            shape((col_count, 2 * width), BF16),
+            shape((CHUNK, 2 * width), F32),
             shape((2, width), F32),
         ],
-        in_specs=[pl.BlockSpec(memory_space=pl.ANY)] + [vmem] * 5,
-        out_specs=[vmem] * 3,
+        in_specs=[vmem, pl.BlockSpec(memory_space=pl.ANY), vmem, vmem],
+        out_specs=[vmem] * 4,
         scratch_shapes=[
+            pltpu.VMEM((row_count, width), BF16),
+            pltpu.VMEM((col_count, width), BF16),
+            pltpu.VMEM((row_count, width), BF16),
+            pltpu.VMEM((col_count, width), BF16),
+            pltpu.VMEM((CHUNK, width), BF16),
+            pltpu.VMEM((CHUNK, width), BF16),
+            pltpu.VMEM((2, 8, width), F32),
+            pltpu.VMEM((row_count, width), BF16),
+            pltpu.VMEM((row_count, width), BF16),
+            pltpu.VMEM((2, 8, width), F32),
+            pltpu.VMEM((width, width), F32),
+            pltpu.VMEM((width, 2 * width), F32),
             pltpu.VMEM((row_count, 2 * width), F32),
             dma,
             pltpu.VMEM((HALF, 2 * HALF), F32),
@@ -550,46 +586,18 @@
             pltpu.VMEM((2 * HALF, HALF), F32),
             pltpu.VMEM((8 * HALF, HALF), F32),
             pltpu.VMEM((80, HALF), F32),
-        ],
-        compiler_params=pltpu.CompilerParams(vmem_limit_bytes=VMEM_LIMIT),
-        name="panels",
-    )(front, rows, cols, corner, prev_pivots.reshape(1, width), pivot_order)
-    chunk, second, shared, new_rows, new_cols = pl.pallas_call(
-        share_kernel,
-        out_shape=[
-            shape((CHUNK, width), BF16),
-            shape((CHUNK, width), BF16),
-            shape((2, width), F32),
-            shape((row_count, width), BF16),
-            shape((col_count, width), BF16),
-        ],
-        in_specs=[vmem] * 3,
-        out_specs=[vmem] * 5,
-        scratch_shapes=Spread.semaphores() + [dma((3, 16)), dma((3,)), dma((3,))],
+            dma((4, 16)),
+            dma((4,)),
+        ]
+        + Spread.semaphores() * 2
+        + Corner.semaphores() * 2,
         compiler_params=pltpu.CompilerParams(
-            collective_id=1, has_side_effects=True, vmem_limit_bytes=VMEM_LIMIT
+            collective_id=0, has_side_effects=True, vmem_limit_bytes=VMEM_LIMIT
         ),
-        name="share",
-    )(left, right, pivot_rows)
-
-    first_row = (g * 16 + r) * row_count
-    row_ids = first_row + lax.broadcasted_iota(jnp.int32, (row_count, 1), 0)
-    col_ids = c * col_count + lax.broadcasted_iota(jnp.int32, (col_count, 1), 0)
-    own_ids = first_row + c * CHUNK + lax.broadcasted_iota(jnp.int32, (CHUNK, 1), 0)
-    none = jnp.zeros((), BF16)
-    new_rows = jnp.where(row_ids >= width, new_rows, none)
-    new_cols = jnp.where(col_ids >= width, new_cols, none)
-    second = jnp.where(own_ids >= width, second, none)
-    scaled = jnp.concatenate(
-        [
-            (rows.astype(F32) * prev_pivots).astype(BF16),
-            (new_rows.astype(F32) * shared[0]).astype(BF16),
-        ],
-        axis=1,
-    )
-    schur = front - times(scaled, jnp.concatenate([cols, new_cols], axis=1), NT)
-    panels = jnp.concatenate([chunk.astype(F32) * shared[0], second.astype(F32) * shared[1]], axis=1)
-    return schur, panels, shared.reshape(2 * width)
+        name="window",
+    )(prev_lower, front, prev_pivots.reshape(1, width), pivot_order)
+    schur = front - times(left_side, right_side, NT)
+    return schur, panels, pivots.reshape(2 * width)
 
 
 def solution(mesh):

time: 107 us -> 79.7 us (0.74)
  Pallas kernels: 99.8 us -> 73.5 us
  other arithmetic: 3.13 us -> 0 us
  matrix products: 2.08 us -> 3.48 us
    pallas_call x3 -> x1, Pallas kernels: 99.8 us -> 73.5 us  [body(): pl.pallas_call(window_kernel, out_shape=[shape((row_count, 2 * width), BF...]
    dot_general x1, matrix products: 2.08 us -> 3.48 us  [times(): lax.dot_general(a, b, (dims, ((), ())), precision=precision, preferred_el...]
    unnamed x15 -> x6, local copies, waits for them, and re-layouts: 0.61 us -> 1.89 us
    select_n x1 -> x0, other arithmetic: 1.24 us -> none  [body(): new_cols = jnp.where(col_ids >= width, new_cols, none)]
    convert_element_type x1 -> x0, other arithmetic: 1.15 us -> none  [body(): (new_rows.astype(F32) * shared[0]).astype(BF16)]
where the time goes in v2:
time: 79.7 us; the launch traced here: 79.5 us
  Pallas kernels  73.5 us (92%)
  matrix products  3.48 us (4%)
  local copies, waits for them, and re-layouts  1.89 us (2%)
    pallas_call x1, Pallas kernels, body(): pl.pallas_call(window_kernel, out_shape=[shape((row_count, 2 * width), BF...  73.5 us
    dot_general x1, matrix products, times(): lax.dot_general(a, b, (dims, ((), ())), precision=precision, preferred_el...  3.48 us
    unnamed x6, local copies, waits for them, and re-layouts  1.89 us

profile of v2, /device:TPU:1, one launch (start us, length us, event | category | flops | bytes accessed | tf_op | source)
XLA Modules:
  0.0 79.5 jit_solution(1059463280056748025)
XLA Ops:
  0.6 0.0 copy-start
  0.6 73.5 %window.1 = (bf16[512,512]{1,0:T(8,128)(2,1)}, bf16[1024,512]{1,0:T(8,128)(2,1)}, f32[32,512]{1,0:T(8,128)}, f32[2,256]{1,0:T(2,128)}) custom-call(bf16[32,256]{1,0:T(8,128)(2,1)} %prev_chunk.1, f32[512,1024]{1,0:T(8,128)} %whole.1, f32[1,256]{1,0:T(1,128)} %bitcast.7, s32[2,256]{1,0:T(2,128)} %orders.1), custom_call_target="tpu_custom_call" | custom-call | tf_op jit(solution)/shard_map/window/pallas_call | solution.py:558
  74.1 1.3 %copy.7 = f32[1,2,2,128]{3,1,2,0:T(2,128)} copy(f32[1,2,2,128]{3,2,1,0:T(2,128)} %bitcast.6) | data formatting | bytes 4096
  75.4 0.0 copy-done
  75.4 0.0 copy-start.1
  75.4 3.5 %convolution_subtract_fusion = f32[512,1024]{1,0:T(8,128)} fusion(f32[512,1024]{1,0:T(8,128)S(1)} %copy-done, bf16[512,512]{1,0:T(8,128)(2,1)} %get-tuple-element.7, bf16[1024,512]{1,0:T(8,128)(2,1)} %get-tuple-element.8), kind=kOutput, calls=%fused_computation | convolution fusion | flops 537395200 | bytes 5767168 | tf_op jit(solution)/shard_map/dot_general | solution.py:295
  78.8 0.0 copy-done.1
  78.8 0.6 copy.9
Async XLA Ops:
  0.6 74.7 %copy-start = (f32[512,1024]{1,0:T(8,128)S(1)}, f32[512,1024]{1,0:T(8,128)}, u32[]{:S(2)}) copy-start(f32[512,1024]{1,0:T(8,128)} %whole.1) | copy-start | bytes 6291460
  75.4 3.5 %copy-start.1 = (f32[32,512]{1,0:T(8,128)S(1)}, f32[32,512]{1,0:T(8,128)}, u32[]{:S(2)}) copy-start(f32[32,512]{1,0:T(8,128)} %get-tuple-element.15) | copy-start | bytes 196612

commit v3 on v2

--- a/solution.py
+++ b/solution.py
@@ -137,7 +137,7 @@
             self.partner(dz, self.yl).start()
         self.own_row_copy().start()
 
-    def first_columns(self):
+    def columns_arrive(self):
         for i in range(4):
             me = self.is_me(self.source(i))
 
@@ -149,9 +149,13 @@
             def _():
                 self.arriving(i).wait_recv()
 
+    def columns_send(self):
         for dx in range(1, 4):
             self.across_x(dx, self.x).start()
         self.sibling(0, self.g).start()
+
+    def urgent(self, grp, dx):
+        return (grp == 0) & (turn(self.x, -dx, 4) < 2)
 
     def pass_rows(self):
         for dz in range(1, 8):
@@ -159,17 +163,25 @@
             if self.full is None:
                 self.partner(dz, self.yl).start()
 
+    def pass_column(self, dx):
+        self.across_x(dx, turn(self.x, -dx, 4)).wait_recv()
+        self.sibling(dx, self.g).start()
+
     def pass_columns(self):
         for dx in range(1, 4):
-            self.across_x(dx, turn(self.x, -dx, 4)).wait_recv()
-            self.sibling(dx, self.g).start()
-
-    def finish(self):
+            self.pass_column(dx)
+
+    def finish_rows(self):
         self.own_row_copy().wait()
         for dz in range(8):
             self.partner(dz, 1 - self.yl).wait_recv()
+
+    def finish_column(self, dx):
+        self.sibling(dx, 1 - self.g).wait_recv()
+
+    def finish_columns(self):
         for dx in range(4):
-            self.sibling(dx, 1 - self.g).wait_recv()
+            self.finish_column(dx)
 
     def drain(self):
         for j in range(4):
@@ -302,79 +314,84 @@
 TN = ((0,), (0,))
 
 
-def eliminate(work, inverse, pivots, recips, columns, small):
-    def panel(first):
-        def step(number, carry):
-            top = pl.multiple_of(number * 8, 8)
-            lane = [jnp.full((8, HALF), top + k, jnp.int32) for k in range(8)]
-            head = work[pl.ds(top, 8), 0:HALF]
+def inverted(value):
+    guess = pl.reciprocal(value, approx=True)
+    guess = guess * (2.0 - value * guess)
+    return guess * (2.0 - value * guess)
+
+
+def eliminate(work, inverse, pivots, recips, columns, small, between=None):
+    parts = (slice(0, HALF), slice(HALF, 2 * HALF))
+    ids = lax.broadcasted_iota(jnp.int32, (8, HALF), 0)
+
+    def spread_lane(tile, lane):
+        return jnp.broadcast_to(tile[:, lane:lane + 1], (8, HALF))
+
+    for number in range(16):
+        if between is not None and number == 8:
+            between()
+        top = 8 * number
+        mine = slice(top, top + 8)
+        at = 256 * (number % 2)
+        head = work[mine, parts[0]]
+        for k in range(8):
+            small[at + 8 * k:at + 8 * k + 8, :] = spread_lane(head, top + k)
+        for i in range(number + 1, 16):
+            tile = work[8 * i:8 * i + 8, parts[0]]
             for k in range(8):
-                small[8 * k:8 * k + 8, :] = jnp.take_along_axis(head, lane[k], axis=1)
-            for i in range(first, 16):
-                tile = work[8 * i:8 * i + 8, 0:HALF]
-                for k in range(8):
-                    columns[8 * (8 * i + k):8 * (8 * i + k) + 8, :] = jnp.take_along_axis(
-                        tile, lane[k], axis=1
-                    )
-            value = {}
-            for k in range(8):
-                for j in range(k, 8):
-                    value[j, k] = jnp.broadcast_to(
-                        small[8 * k + j:8 * k + j + 1, :], (8, HALF)
-                    )
-            small[64:72, :] = head
-            small[72:80, :] = work[pl.ds(top, 8), HALF:2 * HALF]
-            row = [
-                [
-                    jnp.broadcast_to(small[64 + 8 * part + k:65 + 8 * part + k, :], (8, HALF))
-                    for part in range(2)
+                columns[8 * (8 * i + k):8 * (8 * i + k) + 8, :] = spread_lane(tile, top + k)
+        value = {}
+        for k in range(8):
+            for j in range(k, 8):
+                value[j, k] = jnp.broadcast_to(
+                    small[at + 8 * k + j:at + 8 * k + j + 1, :], (8, HALF)
+                )
+        row = [
+            [
+                jnp.broadcast_to(work[top + k:top + k + 1, part], (8, HALF)) for part in parts
+            ]
+            for k in range(8)
+        ]
+        factor = {}
+        recip = []
+        for k in range(8):
+            recip.append(inverted(value[k, k]))
+            for j in range(k + 1, 8):
+                factor[j, k] = value[j, k] * recip[k]
+            for j in range(k + 1, 8):
+                for i in range(j, 8):
+                    value[i, j] = value[i, j] - factor[j, k] * value[i, k]
+                for part in range(2):
+                    row[j][part] = row[j][part] - factor[j, k] * row[k][part]
+        kept = [row[0][1], value[0, 0], recip[0]]
+        for k in range(1, 8):
+            kept[0] = jnp.where(ids == k, row[k][1], kept[0])
+            kept[1] = jnp.where(ids == k, value[k, k], kept[1])
+            kept[2] = jnp.where(ids == k, recip[k], kept[2])
+        inverse[mine, :] = kept[0]
+        pivots[mine, :] = kept[1]
+        recips[mine, :] = kept[2]
+        if number == 15:
+            break
+        for k in range(7, -1, -1):
+            for part in range(2):
+                total = row[k][part] * recip[k]
+                for j in range(k + 1, 8):
+                    total = total - factor[j, k] * row[j][part]
+                row[k][part] = total
+        for i in range(number + 1, 16):
+            rows = slice(8 * i, 8 * i + 8)
+            for part in range(2):
+                terms = [
+                    columns[8 * (8 * i + k):8 * (8 * i + k) + 8, :] * row[k][part]
+                    for k in range(8)
                 ]
-                for k in range(8)
-            ]
-            factor = {}
-            recip = []
-            for k in range(8):
-                recip.append(1.0 / value[k, k])
-                for j in range(k + 1, 8):
-                    factor[j, k] = value[j, k] * recip[k]
-                for j in range(k + 1, 8):
-                    for i in range(j, 8):
-                        value[i, j] = value[i, j] - factor[j, k] * value[i, k]
-                    for part in range(2):
-                        row[j][part] = row[j][part] - factor[j, k] * row[k][part]
-            ids = lax.broadcasted_iota(jnp.int32, (8, HALF), 0)
-            kept = [row[0][1], value[0, 0], recip[0]]
-            for k in range(1, 8):
-                kept[0] = jnp.where(ids == k, row[k][1], kept[0])
-                kept[1] = jnp.where(ids == k, value[k, k], kept[1])
-                kept[2] = jnp.where(ids == k, recip[k], kept[2])
-            inverse[pl.ds(top, 8), :] = kept[0]
-            pivots[pl.ds(top, 8), :] = kept[1]
-            recips[pl.ds(top, 8), :] = kept[2]
-            for k in range(7, -1, -1):
-                for part in range(2):
-                    total = row[k][part] * recip[k]
-                    for j in range(k + 1, 8):
-                        total = total - factor[j, k] * row[j][part]
-                    row[k][part] = total
-            for i in range(first, 16):
-                for part in range(2):
-                    at = (slice(8 * i, 8 * i + 8), slice(part * HALF, (part + 1) * HALF))
-                    total = work[at]
-                    for k in range(8):
-                        total = total - (
-                            columns[8 * (8 * i + k):8 * (8 * i + k) + 8, :] * row[k][part]
-                        )
-                    work[at] = total
-            return carry
-
-        return step
-
-    for quarter in range(4):
-        lax.fori_loop(quarter * 4, quarter * 4 + 4, panel(quarter * 4), 0)
-
-
-def factor(square, order, halfway, work, inverse, pivots, recips, columns, small):
+                while len(terms) > 1:
+                    terms = [x + y for x, y in zip(terms[::2], terms[1::2])]
+                work[rows, parts[part]] = work[rows, parts[part]] - terms[0]
+
+
+def factor(square, order, hooks, work, inverse, pivots, recips, columns, small):
     size = square.shape[0]
     ids = lax.broadcasted_iota(jnp.int32, (size, size), 0)
     chosen = (ids == order).astype(F32)
@@ -387,14 +404,15 @@
     work[:, lo] = moved[lo, lo]
     work[:, hi] = eye
     eliminate(work, inverse.at[lo], pivots.at[lo], recips.at[lo], columns, small)
-    halfway()
+    hooks[0]()
     first = inverse[lo, :]
     upper = times(first, moved[lo, hi], NN, EXACT)
     scaled = upper * recips[lo, :]
     work[:, lo] = moved[hi, hi] - times(scaled, upper, TN, EXACT)
     work[:, hi] = eye
     below = times(scaled, first, TN, EXACT)
-    eliminate(work, inverse.at[hi], pivots.at[hi], recips.at[hi], columns, small)
+    eliminate(work, inverse.at[hi], pivots.at[hi], recips.at[hi], columns, small, hooks[1])
+    hooks[2]()
     second = inverse[hi, :]
     cross = -times(second, below, NN, EXACT)
     top = jnp.concatenate([first * recips[lo, :], jnp.zeros((HALF, HALF), F32)], axis=1)
@@ -404,11 +422,15 @@
     return solver, values
 
 
+def nothing():
+    pass
+
+
 def window_kernel(
-    prev_chunk, whole, prev_pivots, orders,
-    left_side, right_side, panels, pivots_out,
-    rows, cols, new_rows, new_cols, chunk, second, shared,
-    left, right, values, corner, edges, front, landed,
+    chunk_in, whole, pivots_in, orders_in,
+    old_left, old_right, new_left_out, new_right_out, panels_out, pivots_out,
+    prev_chunk, prev_pivots, orders, panels, pivots_kept, given_in, rows, rows_scaled, cols, new_rows, new_left, new_cols, chunk, second, shared,
+    left, right, values, corner, edges, front, landed, stored,
     work, inverse, pivots, recips, columns, small,
     send, recv, *sems,
 ):
@@ -421,6 +443,14 @@
     low_square = Corner(whole, WIDTH, edges, sems[2 * split + deal:])
     scratch = (work, inverse, pivots, recips, columns, small)
     lo, hi = slice(0, WIDTH), slice(WIDTH, 2 * WIDTH)
+    inputs = [
+        pltpu.make_async_copy(source, target, given_in.at[n])
+        for n, (source, target) in enumerate(
+            ((chunk_in, prev_chunk), (pivots_in, prev_pivots), (orders_in, orders))
+        )
+    ]
+    for copy in inputs:
+        copy.start()
 
     def handed(number, panel, to):
         device = (g, r, to)
@@ -431,6 +461,17 @@
         return remote(source, landing, send.at[2 * number + panel, to],
                       recv.at[2 * number + panel], device)
 
+    def keep_old():
+        rows_scaled[...] = (rows[...].astype(F32) * before).astype(BF16)
+
+    keeping = (
+        pltpu.make_async_copy(rows_scaled, old_left, stored.at[0]),
+        pltpu.make_async_copy(cols, old_right, stored.at[1]),
+    )
+    keep_left = pltpu.make_async_copy(new_left, new_left_out, stored.at[2])
+    keep_panels = pltpu.make_async_copy(panels, panels_out, stored.at[4])
+    keep_pivots = pltpu.make_async_copy(pivots_kept, pivots_out, stored.at[5])
+    keep_right = pltpu.make_async_copy(new_cols, new_right_out, stored.at[3])
     barrier = pltpu.get_barrier_semaphore()
     count = old.greet(barrier) + top_square.greet(barrier)
 
@@ -438,7 +479,11 @@
     def _():
         signal(barrier, (g, r, 0))
 
-    pl.semaphore_wait(barrier, count + jnp.where(c == 0, 15, 0))
+    with jax.named_scope("barrier"):
+        pl.semaphore_wait(barrier, count + jnp.where(c == 0, 15, 0))
+    for copy in inputs:
+        copy.wait()
+    before = prev_pivots[...]
     top_square.begin()
     old.begin()
     low_square.begin()
@@ -446,146 +491,337 @@
 
     @pl.when(c == 0)
     def _():
+        new = Spread(block(left, 0, CHUNK), new_rows, new_cols, sems[split:2 * split], left)
         fetch.start()
-        top_square.first_hop()
-
-    old.pass_rows()
-    old.first_columns()
-
-    @pl.when(c == 0)
-    def _():
-        top_square.second_hop()
-
-    old.pass_columns()
-
-    @pl.when(c == 0)
-    def _():
-        top_square.third_hop()
-        low_square.first_hop()
-
-    old.finish()
-    before = prev_pivots[...]
-    rows_scaled = (rows[...].astype(F32) * before).astype(BF16)
-    left_side[:, lo] = rows_scaled
-    right_side[:, lo] = cols[...]
-
-    @pl.when(c == 0)
-    def _():
-        new = Spread(block(left, 0, CHUNK), new_rows, new_cols, sems[split:2 * split], left)
-        near = cols[0:2 * WIDTH, :]
+        with jax.named_scope("top_first"):
+            top_square.first_hop()
+        with jax.named_scope("columns_arrive"):
+            old.columns_arrive()
+
+        @pl.when(old.urgent(g, 0))
+        def _():
+            old.columns_send()
+
+        with jax.named_scope("top_second"):
+            top_square.second_hop()
+        with jax.named_scope("columns_pass"):
+            for dx in range(1, 4):
+                @pl.when(old.urgent(g, dx))
+                def _():
+                    old.pass_column(dx)
+
+        with jax.named_scope("top_third"):
+            top_square.third_hop()
+        with jax.named_scope("columns_finish"):
+            for dx in range(4):
+                @pl.when(old.urgent(1 - g, dx))
+                def _():
+                    old.finish_column(dx)
+
+        @pl.when(jnp.logical_not(old.urgent(g, 0)))
+        def _():
+            old.columns_send()
+
+        with jax.named_scope("low_first"):
+            low_square.first_hop()
+        near = cols[lo, :]
         near_scaled = (near.astype(F32) * before).astype(BF16)
-        both = times(near_scaled[lo], near[lo], NT) + times(near[lo], near_scaled[lo], NT)
-        top_square.finish()
-        solver, given = factor(
-            corner[...] - 0.5 * both, orders[0:1, :], low_square.second_hop, *scratch
-        )
+        both = times(near_scaled, near, NT) + times(near, near_scaled, NT)
+        with jax.named_scope("top_finish"):
+            top_square.finish()
+
+        def middle():
+            with jax.named_scope("hook0"):
+                low_square.second_hop()
+                old.pass_rows()
+
+        def late():
+            with jax.named_scope("hook1"):
+                for dx in range(1, 4):
+                    @pl.when(jnp.logical_not(old.urgent(g, dx)))
+                    def _():
+                        old.pass_column(dx)
+
+        def last():
+            with jax.named_scope("hook2"):
+                low_square.third_hop()
+
+        with jax.named_scope("factor0"):
+            solver, given = factor(
+                corner[...] - 0.5 * both, orders[0:1, :], (middle, late, last), *scratch
+            )
         values[0] = jnp.broadcast_to(given, (8, WIDTH))
-        fetch.wait()
-        panel = front[:, lo] - times(left_side[:, lo], near[lo], NT)
-        shown = times(panel, solver, NT, EXACT).astype(BF16)
-        left[...] = shown
-        low_square.third_hop()
-        low_square.finish()
-        edge = edges[:, lo] - times(near_scaled[hi], near[lo], NT)
-        edge = times(edge, solver, NT, EXACT).astype(BF16)
-        for to in range(1, 16):
-            handed(0, 0, to).start()
-        new.begin()
-        for to in range(1, 16):
-            handed(1, 0, to).start()
-        chunk[...] = left[0:CHUNK, :]
+        with jax.named_scope("wait_rows"):
+            fetch.wait()
+            old.finish_rows()
+        with jax.named_scope("panel0"):
+            keep_old()
+            panel = front[:, lo] - times(rows_scaled[...], near, NT)
+            shown = times(panel, solver, NT, EXACT).astype(BF16)
+            left[...] = shown
+        with jax.named_scope("wait_low"):
+            for dx in range(4):
+                @pl.when(jnp.logical_not(old.urgent(1 - g, dx)))
+                def _():
+                    old.finish_column(dx)
+
+            low_square.finish()
+        with jax.named_scope("edge"):
+            next_near = cols[hi, :]
+            next_scaled = (next_near.astype(F32) * before).astype(BF16)
+            edge = edges[:, lo] - times(next_scaled, near, NT)
+            edge = times(edge, solver, NT, EXACT).astype(BF16)
+        with jax.named_scope("scatter"):
+            for to in range(1, 16):
+                handed(0, 0, to).start()
+            new.begin()
+            for to in range(1, 16):
+                handed(1, 0, to).start()
+            for copy in keeping:
+                copy.start()
         edge_scaled = (edge.astype(F32) * given).astype(BF16)
-        both = times(near_scaled[hi], near[hi], NT) + times(near[hi], near_scaled[hi], NT)
+        both = times(next_scaled, next_near, NT) + times(next_near, next_scaled, NT)
         more = times(edge_scaled, edge, NT) + times(edge, edge_scaled, NT)
         square = (edges[:, hi] - 0.5 * both) - 0.5 * more
-        solver, later = factor(square, orders[1:2, :], lambda: None, *scratch)
+
+        def early_columns():
+            with jax.named_scope("hook3"):
+                new.columns_arrive()
+                new.columns_send()
+
+        def late_columns():
+            with jax.named_scope("hook4"):
+                new.pass_rows()
+
+        with jax.named_scope("factor1"):
+            solver, later = factor(
+                square, orders[1:2, :], (nothing, early_columns, late_columns), *scratch
+            )
         values[1] = jnp.broadcast_to(later, (8, WIDTH))
-        shown_scaled = (left[...].astype(F32) * given).astype(BF16)
-        panel = front[:, hi] - times(left_side[:, lo], near[hi], NT)
-        panel = panel - times(shown_scaled, edge, NT)
-        right[...] = times(panel, solver, NT, EXACT).astype(BF16)
-        new.first_columns()
+        with jax.named_scope("panel1"):
+            shown_scaled = (left[...].astype(F32) * given).astype(BF16)
+            panel = front[:, hi] - times(rows_scaled[...], next_near, NT)
+            panel = panel - times(shown_scaled, edge, NT)
+            right[...] = times(panel, solver, NT, EXACT).astype(BF16)
+        @pl.when(q != 0)
+        def _():
+            new_left[...] = shown_scaled
+
+        @pl.when(q == 0)
+        def _():
+            new_left[lo, :] = jnp.zeros_like(new_left[lo, :])
+            new_left[hi, :] = shown_scaled[hi]
+
+        chunk[...] = left[0:CHUNK, :]
+        shared[...] = values[...]
         for to in range(1, 16):
             handed(1, 1, to).start()
             handed(0, 1, to).start()
         second[...] = right[0:CHUNK, :]
-        shared[...] = values[...]
-        new.pass_rows()
-        new.pass_columns()
-        new.finish()
-        new.drain()
-        for to in range(1, 16):
-            for panel in range(2):
-                handed(0, panel, to).wait_send()
-                handed(1, panel, to).wait_send()
-        top_square.drain()
-        low_square.drain()
+        with jax.named_scope("last_columns"):
+            new.pass_columns()
+        keep_left.start()
+        with jax.named_scope("finish"):
+            new.finish_rows()
+            new.finish_columns()
+        with jax.named_scope("drain"):
+            new.drain()
+        new_cols[lo, :] = jnp.zeros((WIDTH, WIDTH), BF16)
 
     @pl.when(c != 0)
     def _():
+        with jax.named_scope("old"):
+            old.pass_rows()
+            old.columns_arrive()
+            old.columns_send()
+            old.pass_columns()
+            old.finish_rows()
+            old.finish_columns()
+        keep_old()
+        for copy in keeping:
+            copy.start()
         new = Spread(chunk, new_rows, new_cols, sems[split:2 * split])
-        handed(0, 0, c).wait_recv()
+        with jax.named_scope("recv_chunk"):
+            handed(0, 0, c).wait_recv()
         new.begin()
-        new.pass_rows()
-        new.first_columns()
-        new.pass_columns()
-        handed(1, 0, c).wait_recv()
-        handed(1, 1, c).wait_recv()
-        handed(0, 1, c).wait_recv()
-        new.finish()
+        with jax.named_scope("pass_rows"):
+            new.pass_rows()
+        with jax.named_scope("columns_arrive"):
+            new.columns_arrive()
+            new.columns_send()
+        with jax.named_scope("pass_columns"):
+            new.pass_columns()
+        with jax.named_scope("finish_rows"):
+            new.finish_rows()
+            handed(1, 0, c).wait_recv()
+        given = shared[0, 0:1, :]
+
+        @pl.when(q != 0)
+        def _():
+            new_left[...] = (new_rows[...].astype(F32) * given).astype(BF16)
+
+        @pl.when(q == 0)
+        def _():
+            new_left[lo, :] = jnp.zeros_like(new_left[lo, :])
+            new_left[hi, :] = (new_rows[hi, :].astype(F32) * given).astype(BF16)
+
+        keep_left.start()
+        with jax.named_scope("finish_columns"):
+            new.finish_columns()
+        keep_right.start()
+        with jax.named_scope("recv_values"):
+            handed(1, 1, c).wait_recv()
+            handed(0, 1, c).wait_recv()
         new.drain()
 
-    old.drain()
-    row_ids = q * rows.shape[0] + lax.broadcasted_iota(jnp.int32, (rows.shape[0], 1), 0)
-    col_ids = c * cols.shape[0] + lax.broadcasted_iota(jnp.int32, (cols.shape[0], 1), 0)
-    own_ids = q * rows.shape[0] + c * CHUNK + lax.broadcasted_iota(jnp.int32, (CHUNK, 1), 0)
     given, later = shared[0, 0:1, :], shared[1, 0:1, :]
-    live = jnp.where(row_ids >= WIDTH, new_rows[...].astype(F32), 0.0)
-    left_side[:, hi] = (live * given).astype(BF16)
-    right_side[:, hi] = jnp.where(col_ids >= WIDTH, new_cols[...].astype(F32), 0.0).astype(BF16)
     panels[:, lo] = chunk[...].astype(F32) * given
-    panels[:, hi] = jnp.where(own_ids >= WIDTH, second[...].astype(F32), 0.0) * later
-    pivots_out[0:1, :] = given
-    pivots_out[1:2, :] = later
+    live = (q != 0) | (c >= WIDTH // CHUNK)
+
+    @pl.when(live)
+    def _():
+        panels[:, hi] = second[...].astype(F32) * later
+
+    @pl.when(jnp.logical_not(live))
+    def _():
+        panels[:, hi] = jnp.zeros((CHUNK, WIDTH), F32)
+
+    pivots_kept[:, lo] = given
+    pivots_kept[:, hi] = later
+    keep_panels.start()
+    keep_pivots.start()
+    @pl.when(c == 0)
+    def _():
+        keep_right.start()
+        with jax.named_scope("drain_last"):
+            for to in range(1, 16):
+                for panel in range(2):
+                    handed(0, panel, to).wait_send()
+                    handed(1, panel, to).wait_send()
+            top_square.drain()
+            low_square.drain()
+
+    with jax.named_scope("drain_old"):
+        old.drain()
+        for copy in (*keeping, keep_left, keep_right, keep_panels, keep_pivots):
+            copy.wait()
+
+
+def apply_kernel(front, old_left, old_right, new_left, new_right, panels, pivots,
+                 schur, panels_out, pivots_out,
+                 tiles, results, lefts, rights, front_in, sides_in, rights_in, out,
+                 panels_kept, pivots_kept, small_in, small_out):
+    wide = front.shape[1] // TILES
+
+    def near(ref, j):
+        return ref.at[pl.ds(j * wide, wide)]
+
+    sides = [
+        pltpu.make_async_copy(source, lefts.at[n], sides_in.at[n])
+        for n, source in enumerate((old_left, new_left))
+    ]
+    fetches = []
+    for copy in sides:
+        copy.start()
+    for j in range(TILES):
+        across = pl.ds(j * wide, wide)
+        group = [
+            pltpu.make_async_copy(near(source, j), near(rights.at[n], j), rights_in.at[n, j])
+            for n, source in enumerate((old_right, new_right))
+        ]
+        group.append(
+            pltpu.make_async_copy(front.at[:, across], tiles.at[j], front_in.at[j])
+        )
+        for copy in group:
+            copy.start()
+        fetches.append(group)
+    small = (
+        (panels, panels_kept, panels_out),
+        (pivots, pivots_kept, pivots_out),
+    )
+    arrivals = [
+        pltpu.make_async_copy(a, b, small_in.at[n]) for n, (a, b, _) in enumerate(small)
+    ]
+    leaving = [
+        pltpu.make_async_copy(b, c, small_out.at[n]) for n, (_, b, c) in enumerate(small)
+    ]
+    for copy in arrivals:
+        copy.start()
+    for copy in sides:
+        copy.wait()
+    stores = []
+    for j in range(TILES):
+        for copy in fetches[j]:
+            copy.wait()
+        rows = slice(j * wide, (j + 1) * wide)
+        update = times(lefts[0], rights[0, rows, :], NT) + times(lefts[1], rights[1, rows, :], NT)
+        results[j] = tiles[j] - update
+        store = pltpu.make_async_copy(
+            results.at[j], schur.at[:, pl.ds(j * wide, wide)], out.at[j]
+        )
+        store.start()
+        stores.append(store)
+        if j == 0:
+            for copy, onward in zip(arrivals, leaving):
+                copy.wait()
+                onward.start()
+    for store in stores + leaving:
+        store.wait()
+
+
+TILES = 4
 
 
 def body(front, prev_lower, prev_pivots, pivot_order):
     row_count, col_count = front.shape
     width = prev_lower.shape[1]
     vmem = pl.BlockSpec(memory_space=pltpu.VMEM)
+    anywhere = pl.BlockSpec(memory_space=pl.ANY)
     shape = jax.ShapeDtypeStruct
     dma = pltpu.SemaphoreType.DMA
-    left_side, right_side, panels, pivots = pl.pallas_call(
+    scratch = pltpu.VMEM
+    old_left, old_right, new_left, new_right, panels, pivots = pl.pallas_call(
         window_kernel,
         out_shape=[
-            shape((row_count, 2 * width), BF16),
-            shape((col_count, 2 * width), BF16),
+            shape((row_count, width), BF16),
+            shape((col_count, width), BF16),
+            shape((row_count, width), BF16),
+            shape((col_count, width), BF16),
             shape((CHUNK, 2 * width), F32),
-            shape((2, width), F32),
+            shape((1, 2 * width), F32),
         ],
-        in_specs=[vmem, pl.BlockSpec(memory_space=pl.ANY), vmem, vmem],
-        out_specs=[vmem] * 4,
+        in_specs=[anywhere] * 4,
+        out_specs=[anywhere] * 6,
         scratch_shapes=[
-            pltpu.VMEM((row_count, width), BF16),
-            pltpu.VMEM((col_count, width), BF16),
-            pltpu.VMEM((row_count, width), BF16),
-            pltpu.VMEM((col_count, width), BF16),
-            pltpu.VMEM((CHUNK, width), BF16),
-            pltpu.VMEM((CHUNK, width), BF16),
-            pltpu.VMEM((2, 8, width), F32),
-            pltpu.VMEM((row_count, width), BF16),
-            pltpu.VMEM((row_count, width), BF16),
-            pltpu.VMEM((2, 8, width), F32),
-            pltpu.VMEM((width, width), F32),
-            pltpu.VMEM((width, 2 * width), F32),
-            pltpu.VMEM((row_count, 2 * width), F32),
+            scratch((CHUNK, width), BF16),
+            scratch((1, width), F32),
+            scratch(pivot_order.shape, jnp.int32),
+            scratch((CHUNK, 2 * width), F32),
+            scratch((1, 2 * width), F32),
+            dma((3,)),
+            scratch((row_count, width), BF16),
+            scratch((row_count, width), BF16),
+            scratch((col_count, width), BF16),
+            scratch((row_count, width), BF16),
+            scratch((row_count, width), BF16),
+            scratch((col_count, width), BF16),
+            scratch((CHUNK, width), BF16),
+            scratch((CHUNK, width), BF16),
+            scratch((2, 8, width), F32),
+            scratch((row_count, width), BF16),
+            scratch((row_count, width), BF16),
+            scratch((2, 8, width), F32),
+            scratch((width, width), F32),
+            scratch((width, 2 * width), F32),
+            scratch((row_count, 2 * width), F32),
             dma,
-            pltpu.VMEM((HALF, 2 * HALF), F32),
-            pltpu.VMEM((2 * HALF, HALF), F32),
-            pltpu.VMEM((2 * HALF, HALF), F32),
-            pltpu.VMEM((2 * HALF, HALF), F32),
-            pltpu.VMEM((8 * HALF, HALF), F32),
-            pltpu.VMEM((80, HALF), F32),
+            dma((6,)),
+            scratch((HALF, 2 * HALF), F32),
+            scratch((2 * HALF, HALF), F32),
+            scratch((2 * HALF, HALF), F32),
+            scratch((2 * HALF, HALF), F32),
+            scratch((8 * HALF, HALF), F32),
+            scratch((320, HALF), F32),
             dma((4, 16)),
             dma((4,)),
         ]
@@ -596,7 +832,33 @@
         ),
         name="window",
     )(prev_lower, front, prev_pivots.reshape(1, width), pivot_order)
-    schur = front - times(left_side, right_side, NT)
+    tile = col_count // TILES
+    schur, panels, pivots = pl.pallas_call(
+        apply_kernel,
+        out_shape=[
+            shape((row_count, col_count), F32),
+            shape((CHUNK, 2 * width), F32),
+            shape((1, 2 * width), F32),
+        ],
+        in_specs=[anywhere] * 7,
+        out_specs=[anywhere] * 3,
+        scratch_shapes=[
+            scratch((TILES, row_count, tile), F32),
+            scratch((TILES, row_count, tile), F32),
+            scratch((2, row_count, width), BF16),
+            scratch((2, col_count, width), BF16),
+            dma((TILES,)),
+            dma((2,)),
+            dma((2, TILES)),
+            dma((TILES,)),
+            scratch((CHUNK, 2 * width), F32),
+            scratch((1, 2 * width), F32),
+            dma((2,)),
+            dma((2,)),
+        ],
+        compiler_params=pltpu.CompilerParams(vmem_limit_bytes=VMEM_LIMIT),
+        name="apply",
+    )(front, old_left, old_right, new_left, new_right, panels, pivots)
     return schur, panels, pivots.reshape(2 * width)
 
 

time: 79.7 us -> 71.8 us (0.901)
  matrix products: 3.48 us -> 0 us
  Pallas kernels: 73.5 us -> 70.2 us
  local copies, waits for them, and re-layouts: 1.89 us -> 0 us
    dot_general x1 -> x0, matrix products: 3.48 us -> none  [times(): lax.dot_general(a, b, (dims, ((), ())), precision=precision, preferred_el...]
    pallas_call x1 -> x2, Pallas kernels: 73.5 us -> 70.2 us  [the longest x1 65.5 us: body(): pl.pallas_call(window_kernel, out_shape=[shape((row_count, width), BF16),...]
    unnamed x6 -> x0, local copies, waits for them, and re-layouts: 1.89 us -> none
where the time goes in v3:
time: 71.8 us; the launch traced here: 71.1 us
  Pallas kernels  70.2 us (98%)
  between operations  0.82 us (1%)
    pallas_call x1, Pallas kernels, body(): pl.pallas_call(window_kernel, out_shape=[shape((row_count, width), BF16),...  65.5 us
    pallas_call x1, Pallas kernels, body(): pl.pallas_call(apply_kernel, out_shape=[shape((row_count, col_count), F32...  4.74 us

profile of v3, /device:TPU:1, one launch (start us, length us, event | category | flops | bytes accessed | tf_op | source)
XLA Modules:
  0.0 71.1 jit_solution(13783780160097610082)
XLA Ops:
  0.6 65.5 %window.1 = (bf16[512,256]{1,0:T(8,128)(2,1)}, bf16[1024,256]{1,0:T(8,128)(2,1)}, bf16[512,256]{1,0:T(8,128)(2,1)}, bf16[1024,256]{1,0:T(8,128)(2,1)}, f32[32,512]{1,0:T(8,128)}, /*index=5*/f32[1,512]{1,0:T(1,128)}) custom-call(bf16[32,256]{1,0:T(8,128)(2,1)} %chunk_in.1, f32[512,1024]{1,0:T(8,128)} %front.1, f32[1,256]{1,0:T(1,128)} %bitcast.2, ...), custom_call_target="tpu_custom_call" | custom-call | tf_op jit(solution)/shard_map/window/pallas_call | solution.py:783
  66.1 4.7 %apply.1 = (f32[512,1024]{1,0:T(8,128)}, f32[32,512]{1,0:T(8,128)}, f32[1,512]{1,0:T(1,128)}) custom-call(f32[512,1024]{1,0:T(8,128)} %front.1, bf16[512,256]{1,0:T(8,128)(2,1)} %get-tuple-element.12.old_left, bf16[1024,256]{1,0:T(8,128)(2,1)} %get-tuple-element.13.old_right, bf16[512,256]{1,0:T(8,128)(2,1)} %get-tuple-element.14.new_left, ...), custom_call_target="tpu_custom_call" | custom-call | tf_op jit(solution)/shard_map/apply/pallas_call | solution.py:836

commit v4 on v3

--- a/solution.py
+++ b/solution.py
@@ -12,6 +12,7 @@
 CHUNK = 32
 WIDTH = 256
 HALF = 128
+TILES = 4
 VMEM_LIMIT = 60 * 1024 * 1024
 
 
@@ -39,8 +40,9 @@
 
 
 class Spread:
-    def __init__(self, chunk, rows, cols, sems, full=None):
+    def __init__(self, chunk, rows, cols, sems, full=None, lean=False):
         self.chunk, self.rows, self.cols, self.full = chunk, rows, cols, full
+        self.lean = lean
         (self.zs, self.zr, self.fs, self.fr, self.ps, self.pr,
          self.xs, self.xr, self.cs, self.cr, self.own) = sems
         g, r, c = place()
@@ -50,8 +52,8 @@
     @staticmethod
     def semaphores():
         dma = pltpu.SemaphoreType.DMA
-        return [dma((7,)), dma((7,)), dma((8,)), dma((8,)), dma((4,)), dma((4,)),
-                dma((3,)), dma((3,)), dma((4,)), dma((4,)), dma((2,))]
+        return [dma, dma((7,)), dma, dma((8,)), dma((4,)), dma((4,)),
+                dma, dma((3,)), dma, dma((4,)), dma((2,))]
 
     def target(self, j):
         return (self.r % 2, (self.c // 4) * 4 + j, self.g * 8 + self.r // 2)
@@ -97,24 +99,24 @@
 
     def across_z(self, dz, slot_z):
         return remote(self.chunk, block(self.rows, self.yl * 8 + slot_z, CHUNK),
-                      self.zs.at[dz - 1], self.zr.at[dz - 1],
+                      self.zs, self.zr.at[dz - 1],
                       (self.g, self.r, self.yl * 8 + turn(self.z, dz, 8)))
 
     def partner(self, dz, side):
         slot = side * 8 + turn(self.z, -dz, 8)
         held = self.rows if self.full is None else self.full
         src = self.chunk if dz == 0 else block(held, slot, CHUNK)
-        return remote(src, block(self.rows, slot, CHUNK), self.fs.at[dz], self.fr.at[dz],
+        return remote(src, block(self.rows, slot, CHUNK), self.fs, self.fr.at[dz],
                       (self.g, self.r, (1 - self.yl) * 8 + self.z))
 
     def across_x(self, dx, x):
         part = block(self.cols, self.g * 4 + x, 4 * CHUNK)
-        return remote(part, part, self.xs.at[dx - 1], self.xr.at[dx - 1],
+        return remote(part, part, self.xs, self.xr.at[dx - 1],
                       (self.g, turn(self.x, dx, 4) * 4 + self.yh, self.c))
 
     def sibling(self, dx, grp):
         part = block(self.cols, grp * 4 + turn(self.x, -dx, 4), 4 * CHUNK)
-        return remote(part, part, self.cs.at[dx], self.cr.at[dx], (1 - self.g, self.r, self.c))
+        return remote(part, part, self.cs, self.cr.at[dx], (1 - self.g, self.r, self.c))
 
     def own_row_copy(self):
         return pltpu.make_async_copy(self.chunk, block(self.rows, self.c, CHUNK), self.own.at[1])
@@ -132,9 +134,14 @@
                 self.crossing(j).start()
 
         for dz in range(1, 8):
-            self.across_z(dz, self.z).start()
+            if self.lean:
+                @pl.when((self.yl != 0) | (turn(self.z, dz, 8) != 0))
+                def _():
+                    self.across_z(dz, self.z).start()
+            else:
+                self.across_z(dz, self.z).start()
         for dz in range(1 if self.full is None else 8):
-            self.partner(dz, self.yl).start()
+            self.pass_to_partner(dz)
         self.own_row_copy().start()
 
     def columns_arrive(self):
@@ -160,8 +167,15 @@
     def pass_rows(self):
         for dz in range(1, 8):
             self.across_z(dz, turn(self.z, -dz, 8)).wait_recv()
-            if self.full is None:
+            self.pass_to_partner(dz)
+
+    def pass_to_partner(self, dz):
+        if self.lean:
+            @pl.when(self.c != 8)
+            def _():
                 self.partner(dz, self.yl).start()
+        else:
+            self.partner(dz, self.yl).start()
 
     def pass_column(self, dx):
         self.across_x(dx, turn(self.x, -dx, 4)).wait_recv()
@@ -183,20 +197,35 @@
         for dx in range(4):
             self.finish_column(dx)
 
+    def sent(self, part, sem):
+        remote(part, part, sem, self.own.at[0], (1 - self.g, self.r, self.c)).wait_send()
+
     def drain(self):
         for j in range(4):
             @pl.when(jnp.logical_not(self.is_me(self.target(j))))
             def _():
                 self.crossing(j).wait_send()
 
-        for dz in range(1, 8):
-            self.across_z(dz, self.z).wait_send()
-        for dz in range(8):
-            self.partner(dz, self.yl).wait_send()
-        for dx in range(1, 4):
-            self.across_x(dx, self.x).wait_send()
-        for dx in range(4):
-            self.sibling(dx, self.g).wait_send()
+        if not self.lean:
+            self.sent(self.rows.at[0:7 * CHUNK], self.zs)
+            self.sent(self.rows.at[0:8 * CHUNK], self.fs)
+            return
+
+        @pl.when((self.yl == 0) & (self.z != 0))
+        def _():
+            self.sent(self.rows.at[0:6 * CHUNK], self.zs)
+
+        @pl.when((self.yl != 0) | (self.z == 0))
+        def _():
+            self.sent(self.rows.at[0:7 * CHUNK], self.zs)
+
+        @pl.when(self.c != 8)
+        def _():
+            self.sent(self.rows.at[0:8 * CHUNK], self.fs)
+
+    def drain_columns(self):
+        self.sent(self.cols.at[0:12 * CHUNK], self.xs)
+        self.sent(self.cols.at[0:16 * CHUNK], self.cs)
 
 
 class Corner:
@@ -212,7 +241,7 @@
     @staticmethod
     def semaphores():
         dma = pltpu.SemaphoreType.DMA
-        return [dma((32,)), dma, dma((3,)), dma((3,)), dma((3,)), dma((3,)), dma((4,)), dma((4,))]
+        return [dma, dma, dma, dma((3,)), dma, dma((3,)), dma, dma((4,))]
 
     def greet(self, barrier):
         @pl.when(self.c == 0)
@@ -231,7 +260,7 @@
         return self.front.at[pl.ds(start, self.rows), pl.ds(0, self.lanes)]
 
     def handing(self, slot):
-        return remote(self.piece(slot), block(self.corner, slot, self.rows), self.ts.at[slot],
+        return remote(self.piece(slot), block(self.corner, slot, self.rows), self.ts,
                       self.tr, (slot // 16, slot % 16, 0))
 
     def keeping(self):
@@ -239,17 +268,17 @@
 
     def across_y(self, dy, yh):
         part = block(self.corner, self.g * 16 + self.x * 4 + yh, self.rows)
-        return remote(part, part, self.ys.at[dy - 1], self.yr.at[dy - 1],
+        return remote(part, part, self.ys, self.yr.at[dy - 1],
                       (self.g, self.x * 4 + turn(self.yh, dy, 4), self.c))
 
     def across_x(self, dx, x):
         part = block(self.corner, self.g * 4 + x, 4 * self.rows)
-        return remote(part, part, self.xs.at[dx - 1], self.xr.at[dx - 1],
+        return remote(part, part, self.xs, self.xr.at[dx - 1],
                       (self.g, turn(self.x, dx, 4) * 4 + self.yh, self.c))
 
     def sibling(self, dx, grp):
         part = block(self.corner, grp * 4 + turn(self.x, -dx, 4), 4 * self.rows)
-        return remote(part, part, self.cs.at[dx], self.cr.at[dx], (1 - self.g, self.r, self.c))
+        return remote(part, part, self.cs, self.cr.at[dx], (1 - self.g, self.r, self.c))
 
     def begin(self):
         @pl.when((self.q == 0) & (self.c == 0))
@@ -291,16 +320,14 @@
     def drain(self):
         @pl.when(self.q == 0)
         def _():
-            @pl.loop(1, 32)
-            def _(slot):
-                self.handing(slot).wait_send()
-
-        for dy in range(1, 4):
-            self.across_y(dy, self.yh).wait_send()
-        for dx in range(1, 4):
-            self.across_x(dx, self.x).wait_send()
-        for dx in range(4):
-            self.sibling(dx, self.g).wait_send()
+            rest = pl.ds(self.rows, 31 * self.rows)
+            start = pl.multiple_of(self.first + self.rows, self.rows)
+            source = self.front.at[pl.ds(start, 31 * self.rows), pl.ds(0, self.lanes)]
+            remote(source, self.corner.at[rest], self.ts, self.tr, (1, 0, 0)).wait_send()
+
+        for part, sem in ((3, self.ys), (12, self.xs), (16, self.cs)):
+            held = self.corner.at[pl.ds(0, part * self.rows)]
+            remote(held, held, sem, self.tr, (1 - self.g, self.r, self.c)).wait_send()
 
 
 def times(a, b, dims, precision=None):
@@ -316,13 +343,57 @@
 
 def inverted(value):
     guess = pl.reciprocal(value, approx=True)
-    guess = guess * (2.0 - value * guess)
     return guess * (2.0 - value * guess)
+
+
+def panel_rows(value, row):
+    ids = lax.broadcasted_iota(jnp.int32, (8, HALF), 0)
+    multiplier = {}
+    turned = {}
+    kept = [None, None, None]
+
+    def keep(k, items):
+        for n, item in enumerate(items):
+            kept[n] = item if kept[n] is None else jnp.where(ids == k, item, kept[n])
+
+    for k in range(0, 8, 2):
+        m = k + 1
+        a, b, c = value[k, k], value[m, k], value[m, m]
+        scale = inverted(a * c - b * b)
+        for j in range(k + 2, 8):
+            x, y = value[j, k], value[j, m]
+            multiplier[j, k] = (c * x - b * y) * scale
+            multiplier[j, m] = (a * y - b * x) * scale
+        for j in range(k + 2, 8):
+            for i in range(j, 8):
+                value[i, j] = value[i, j] - (
+                    multiplier[j, k] * value[i, k] + multiplier[j, m] * value[i, m]
+                )
+            for part in range(2):
+                row[j][part] = row[j][part] - (
+                    multiplier[j, k] * row[k][part] + multiplier[j, m] * row[m][part]
+                )
+        for part in range(2):
+            x, y = row[k][part], row[m][part]
+            turned[k, part] = (c * x - b * y) * scale
+            turned[m, part] = (a * y - b * x) * scale
+        first = inverted(a)
+        ratio = b * first
+        second = c - b * ratio
+        keep(k, (row[k][1], a, first))
+        keep(m, (row[m][1] - ratio * row[k][1], second, inverted(second)))
+    for k in range(6, -1, -2):
+        for m in (k, k + 1):
+            for part in range(2):
+                total = turned[m, part]
+                for j in range(7, k + 1, -1):
+                    total = total - multiplier[j, m] * turned[j, part]
+                turned[m, part] = total
+    return kept, turned
 
 
 def eliminate(work, inverse, pivots, recips, columns, small, between=None):
     parts = (slice(0, HALF), slice(HALF, 2 * HALF))
-    ids = lax.broadcasted_iota(jnp.int32, (8, HALF), 0)
 
     def spread_lane(tile, lane):
         return jnp.broadcast_to(tile[:, lane:lane + 1], (8, HALF))
@@ -332,58 +403,37 @@
             between()
         top = 8 * number
         mine = slice(top, top + 8)
-        at = 256 * (number % 2)
+        at = 64 * (number % 2)
         head = work[mine, parts[0]]
         for k in range(8):
             small[at + 8 * k:at + 8 * k + 8, :] = spread_lane(head, top + k)
         for i in range(number + 1, 16):
             tile = work[8 * i:8 * i + 8, parts[0]]
+            if i == number + 1:
+                soon = [spread_lane(tile, top + k) for k in range(8)]
+                continue
             for k in range(8):
                 columns[8 * (8 * i + k):8 * (8 * i + k) + 8, :] = spread_lane(tile, top + k)
-        value = {}
-        for k in range(8):
-            for j in range(k, 8):
-                value[j, k] = jnp.broadcast_to(
-                    small[at + 8 * k + j:at + 8 * k + j + 1, :], (8, HALF)
-                )
+        value = {
+            (j, k): jnp.broadcast_to(
+                small[at + 8 * k + j:at + 8 * k + j + 1, :], (8, HALF)
+            )
+            for k in range(8) for j in range(k, 8)
+        }
         row = [
-            [
-                jnp.broadcast_to(work[top + k:top + k + 1, part], (8, HALF)) for part in parts
-            ]
+            [jnp.broadcast_to(work[top + k:top + k + 1, part], (8, HALF)) for part in parts]
             for k in range(8)
         ]
-        factor = {}
-        recip = []
-        for k in range(8):
-            recip.append(inverted(value[k, k]))
-            for j in range(k + 1, 8):
-                factor[j, k] = value[j, k] * recip[k]
-            for j in range(k + 1, 8):
-                for i in range(j, 8):
-                    value[i, j] = value[i, j] - factor[j, k] * value[i, k]
-                for part in range(2):
-                    row[j][part] = row[j][part] - factor[j, k] * row[k][part]
-        kept = [row[0][1], value[0, 0], recip[0]]
-        for k in range(1, 8):
-            kept[0] = jnp.where(ids == k, row[k][1], kept[0])
-            kept[1] = jnp.where(ids == k, value[k, k], kept[1])
-            kept[2] = jnp.where(ids == k, recip[k], kept[2])
+        kept, turned = panel_rows(value, row)
         inverse[mine, :] = kept[0]
         pivots[mine, :] = kept[1]
         recips[mine, :] = kept[2]
-        if number == 15:
-            break
-        for k in range(7, -1, -1):
-            for part in range(2):
-                total = row[k][part] * recip[k]
-                for j in range(k + 1, 8):
-                    total = total - factor[j, k] * row[j][part]
-                row[k][part] = total
         for i in range(number + 1, 16):
             rows = slice(8 * i, 8 * i + 8)
             for part in range(2):
                 terms = [
-                    columns[8 * (8 * i + k):8 * (8 * i + k) + 8, :] * row[k][part]
+                    (soon[k] if i == number + 1 else
+                     columns[8 * (8 * i + k):8 * (8 * i + k) + 8, :]) * turned[k, part]
                     for k in range(8)
                 ]
                 while len(terms) > 1:
@@ -428,9 +478,9 @@
 
 def window_kernel(
     chunk_in, whole, pivots_in, orders_in,
-    old_left, old_right, new_left_out, new_right_out, panels_out, pivots_out,
+    updated_out, new_left_out, new_right_out, panels_out, pivots_out,
     prev_chunk, prev_pivots, orders, panels, pivots_kept, given_in, rows, rows_scaled, cols, new_rows, new_left, new_cols, chunk, second, shared,
-    left, right, values, corner, edges, front, landed, stored,
+    left, right, values, corner, edges, front, landed, kept, stored,
     work, inverse, pivots, recips, columns, small,
     send, recv, *sems,
 ):
@@ -457,21 +507,40 @@
         if number == 0:
             source, landing = block((left, right)[panel], to, CHUNK), (chunk, second)[panel]
         else:
-            source, landing = values.at[panel], shared.at[panel]
-        return remote(source, landing, send.at[2 * number + panel, to],
+            source = values.at[panel, pl.ds(pl.multiple_of(to * 8, 8), 8)]
+            landing = shared.at[panel]
+        return remote(source, landing, send.at[2 * number + panel],
                       recv.at[2 * number + panel], device)
 
     def keep_old():
         rows_scaled[...] = (rows[...].astype(F32) * before).astype(BF16)
 
-    keeping = (
-        pltpu.make_async_copy(rows_scaled, old_left, stored.at[0]),
-        pltpu.make_async_copy(cols, old_right, stored.at[1]),
-    )
+    wide = front.shape[1] // TILES
+    keeping = [
+        pltpu.make_async_copy(
+            front.at[:, pl.ds(j * wide, wide)], updated_out.at[:, pl.ds(j * wide, wide)],
+            kept.at[j],
+        )
+        for j in range(TILES)
+    ]
+
+    def apply_old():
+        for j in range(TILES):
+            at = slice(j * wide, (j + 1) * wide)
+            front[:, at] = front[:, at] - times(rows_scaled[...], cols[at, :], NT)
+            keeping[j].start()
+
     keep_left = pltpu.make_async_copy(new_left, new_left_out, stored.at[2])
     keep_panels = pltpu.make_async_copy(panels, panels_out, stored.at[4])
     keep_pivots = pltpu.make_async_copy(pivots_kept, pivots_out, stored.at[5])
     keep_right = pltpu.make_async_copy(new_cols, new_right_out, stored.at[3])
+    keep_near, keep_far = (
+        pltpu.make_async_copy(
+            new_cols.at[pl.ds(n * 2 * WIDTH, 2 * WIDTH)],
+            new_right_out.at[pl.ds(n * 2 * WIDTH, 2 * WIDTH)], stored.at[n],
+        )
+        for n in range(2)
+    )
     barrier = pltpu.get_barrier_semaphore()
     count = old.greet(barrier) + top_square.greet(barrier)
 
@@ -487,12 +556,12 @@
     top_square.begin()
     old.begin()
     low_square.begin()
-    fetch = pltpu.make_async_copy(whole.at[:, 0:2 * WIDTH], front, landed)
+    fetch = pltpu.make_async_copy(whole, front, landed)
+    fetch.start()
 
     @pl.when(c == 0)
     def _():
-        new = Spread(block(left, 0, CHUNK), new_rows, new_cols, sems[split:2 * split], left)
-        fetch.start()
+        new = Spread(block(left, 0, CHUNK), new_rows, new_cols, sems[split:2 * split], left, True)
         with jax.named_scope("top_first"):
             top_square.first_hop()
         with jax.named_scope("columns_arrive"):
@@ -548,9 +617,10 @@
 
         with jax.named_scope("factor0"):
             solver, given = factor(
-                corner[...] - 0.5 * both, orders[0:1, :], (middle, late, last), *scratch
+                corner[...] - 0.5 * both, orders[0:1, :], (middle, late, nothing), *scratch
             )
-        values[0] = jnp.broadcast_to(given, (8, WIDTH))
+        values[0] = jnp.broadcast_to(given, (128, WIDTH))
+        last()
         with jax.named_scope("wait_rows"):
             fetch.wait()
             old.finish_rows()
@@ -577,27 +647,16 @@
             new.begin()
             for to in range(1, 16):
                 handed(1, 0, to).start()
-            for copy in keeping:
-                copy.start()
         edge_scaled = (edge.astype(F32) * given).astype(BF16)
         both = times(next_scaled, next_near, NT) + times(next_near, next_scaled, NT)
         more = times(edge_scaled, edge, NT) + times(edge, edge_scaled, NT)
         square = (edges[:, hi] - 0.5 * both) - 0.5 * more
 
-        def early_columns():
-            with jax.named_scope("hook3"):
-                new.columns_arrive()
-                new.columns_send()
-
-        def late_columns():
-            with jax.named_scope("hook4"):
-                new.pass_rows()
-
         with jax.named_scope("factor1"):
             solver, later = factor(
-                square, orders[1:2, :], (nothing, early_columns, late_columns), *scratch
+                square, orders[1:2, :], (nothing, nothing, nothing), *scratch
             )
-        values[1] = jnp.broadcast_to(later, (8, WIDTH))
+        values[1] = jnp.broadcast_to(later, (128, WIDTH))
         with jax.named_scope("panel1"):
             shown_scaled = (left[...].astype(F32) * given).astype(BF16)
             panel = front[:, hi] - times(rows_scaled[...], next_near, NT)
@@ -613,20 +672,34 @@
             new_left[hi, :] = shown_scaled[hi]
 
         chunk[...] = left[0:CHUNK, :]
-        shared[...] = values[...]
+        shared[...] = values[:, 0:8, :]
         for to in range(1, 16):
             handed(1, 1, to).start()
             handed(0, 1, to).start()
         second[...] = right[0:CHUNK, :]
+        with jax.named_scope("apply_old"):
+            apply_old()
+        with jax.named_scope("arrive"):
+            new.columns_arrive()
+
+        @pl.when(g == 1)
+        def _():
+            new.columns_send()
+
+        new_cols[lo, :] = jnp.zeros((WIDTH, WIDTH), BF16)
+        new_cols[hi, :] = edge
+        keep_near.start()
+        keep_left.start()
         with jax.named_scope("last_columns"):
-            new.pass_columns()
-        keep_left.start()
-        with jax.named_scope("finish"):
-            new.finish_rows()
-            new.finish_columns()
-        with jax.named_scope("drain"):
-            new.drain()
-        new_cols[lo, :] = jnp.zeros((WIDTH, WIDTH), BF16)
+            @pl.when(g == 1)
+            def _():
+                new.pass_columns()
+
+            @pl.when(g == 0)
+            def _():
+                new.finish_columns()
+
+        keep_far.start()
 
     @pl.when(c != 0)
     def _():
@@ -638,9 +711,9 @@
             old.finish_rows()
             old.finish_columns()
         keep_old()
-        for copy in keeping:
-            copy.start()
-        new = Spread(chunk, new_rows, new_cols, sems[split:2 * split])
+        fetch.wait()
+        apply_old()
+        new = Spread(chunk, new_rows, new_cols, sems[split:2 * split], None, True)
         with jax.named_scope("recv_chunk"):
             handed(0, 0, c).wait_recv()
         new.begin()
@@ -673,6 +746,7 @@
             handed(1, 1, c).wait_recv()
             handed(0, 1, c).wait_recv()
         new.drain()
+        new.drain_columns()
 
     given, later = shared[0, 0:1, :], shared[1, 0:1, :]
     panels[:, lo] = chunk[...].astype(F32) * given
@@ -692,45 +766,49 @@
     keep_pivots.start()
     @pl.when(c == 0)
     def _():
-        keep_right.start()
+        new = Spread(block(left, 0, CHUNK), new_rows, new_cols, sems[split:2 * split], left, True)
         with jax.named_scope("drain_last"):
-            for to in range(1, 16):
-                for panel in range(2):
-                    handed(0, panel, to).wait_send()
-                    handed(1, panel, to).wait_send()
+            new.own_row_copy().wait()
+            new.drain()
+
+            @pl.when(g == 1)
+            def _():
+                new.drain_columns()
+
+            for panel in range(2):
+                rest = (left, right)[panel].at[CHUNK:16 * CHUNK]
+                remote(rest, rest, send.at[panel], recv.at[panel], (1 - g, r, c)).wait_send()
+                rest = values.at[panel, 8:128]
+                remote(rest, rest, send.at[2 + panel], recv.at[2 + panel], (1 - g, r, c)).wait_send()
             top_square.drain()
             low_square.drain()
+            keep_near.wait()
+            keep_far.wait()
+
+    @pl.when(c != 0)
+    def _():
+        keep_right.wait()
 
     with jax.named_scope("drain_old"):
         old.drain()
-        for copy in (*keeping, keep_left, keep_right, keep_panels, keep_pivots):
+        old.drain_columns()
+        for copy in (*keeping, keep_left, keep_panels, keep_pivots):
             copy.wait()
 
 
-def apply_kernel(front, old_left, old_right, new_left, new_right, panels, pivots,
+def apply_kernel(front, new_left, new_right, panels, pivots,
                  schur, panels_out, pivots_out,
-                 tiles, results, lefts, rights, front_in, sides_in, rights_in, out,
+                 tiles, results, left, right, front_in, left_in, right_in, out,
                  panels_kept, pivots_kept, small_in, small_out):
     wide = front.shape[1] // TILES
-
-    def near(ref, j):
-        return ref.at[pl.ds(j * wide, wide)]
-
-    sides = [
-        pltpu.make_async_copy(source, lefts.at[n], sides_in.at[n])
-        for n, source in enumerate((old_left, new_left))
-    ]
+    side = pltpu.make_async_copy(new_left, left, left_in)
+    side.start()
     fetches = []
-    for copy in sides:
-        copy.start()
     for j in range(TILES):
-        across = pl.ds(j * wide, wide)
-        group = [
-            pltpu.make_async_copy(near(source, j), near(rights.at[n], j), rights_in.at[n, j])
-            for n, source in enumerate((old_right, new_right))
-        ]
-        group.append(
-            pltpu.make_async_copy(front.at[:, across], tiles.at[j], front_in.at[j])
+        at = pl.ds(j * wide, wide)
+        group = (
+            pltpu.make_async_copy(new_right.at[at], right.at[at], right_in.at[j]),
+            pltpu.make_async_copy(front.at[:, at], tiles.at[j], front_in.at[j]),
         )
         for copy in group:
             copy.start()
@@ -747,15 +825,13 @@
     ]
     for copy in arrivals:
         copy.start()
-    for copy in sides:
-        copy.wait()
+    side.wait()
     stores = []
     for j in range(TILES):
         for copy in fetches[j]:
             copy.wait()
         rows = slice(j * wide, (j + 1) * wide)
-        update = times(lefts[0], rights[0, rows, :], NT) + times(lefts[1], rights[1, rows, :], NT)
-        results[j] = tiles[j] - update
+        results[j] = tiles[j] - times(left[...], right[rows, :], NT)
         store = pltpu.make_async_copy(
             results.at[j], schur.at[:, pl.ds(j * wide, wide)], out.at[j]
         )
@@ -769,9 +845,6 @@
         store.wait()
 
 
-TILES = 4
-
-
 def body(front, prev_lower, prev_pivots, pivot_order):
     row_count, col_count = front.shape
     width = prev_lower.shape[1]
@@ -780,18 +853,17 @@
     shape = jax.ShapeDtypeStruct
     dma = pltpu.SemaphoreType.DMA
     scratch = pltpu.VMEM
-    old_left, old_right, new_left, new_right, panels, pivots = pl.pallas_call(
+    updated, new_left, new_right, panels, pivots = pl.pallas_call(
         window_kernel,
         out_shape=[
-            shape((row_count, width), BF16),
-            shape((col_count, width), BF16),
+            shape((row_count, col_count), F32),
             shape((row_count, width), BF16),
             shape((col_count, width), BF16),
             shape((CHUNK, 2 * width), F32),
             shape((1, 2 * width), F32),
         ],
         in_specs=[anywhere] * 4,
-        out_specs=[anywhere] * 6,
+        out_specs=[anywhere] * 5,
         scratch_shapes=[
             scratch((CHUNK, width), BF16),
             scratch((1, width), F32),
@@ -810,19 +882,20 @@
             scratch((2, 8, width), F32),
             scratch((row_count, width), BF16),
             scratch((row_count, width), BF16),
-            scratch((2, 8, width), F32),
+            scratch((2, 128, width), F32),
             scratch((width, width), F32),
             scratch((width, 2 * width), F32),
-            scratch((row_count, 2 * width), F32),
+            scratch((row_count, col_count), F32),
             dma,
+            dma((TILES,)),
             dma((6,)),
             scratch((HALF, 2 * HALF), F32),
             scratch((2 * HALF, HALF), F32),
             scratch((2 * HALF, HALF), F32),
             scratch((2 * HALF, HALF), F32),
             scratch((8 * HALF, HALF), F32),
-            scratch((320, HALF), F32),
-            dma((4, 16)),
+            scratch((HALF, HALF), F32),
+            dma((4,)),
             dma((4,)),
         ]
         + Spread.semaphores() * 2
@@ -840,16 +913,16 @@
             shape((CHUNK, 2 * width), F32),
             shape((1, 2 * width), F32),
         ],
-        in_specs=[anywhere] * 7,
+        in_specs=[anywhere] * 5,
         out_specs=[anywhere] * 3,
         scratch_shapes=[
             scratch((TILES, row_count, tile), F32),
             scratch((TILES, row_count, tile), F32),
-            scratch((2, row_count, width), BF16),
-            scratch((2, col_count, width), BF16),
+            scratch((row_count, width), BF16),
+            scratch((col_count, width), BF16),
             dma((TILES,)),
-            dma((2,)),
-            dma((2, TILES)),
+            dma,
+            dma((TILES,)),
             dma((TILES,)),
             scratch((CHUNK, 2 * width), F32),
             scratch((1, 2 * width), F32),
@@ -858,7 +931,7 @@
         ],
         compiler_params=pltpu.CompilerParams(vmem_limit_bytes=VMEM_LIMIT),
         name="apply",
-    )(front, old_left, old_right, new_left, new_right, panels, pivots)
+    )(updated, new_left, new_right, panels, pivots)
     return schur, panels, pivots.reshape(2 * width)
 
 

time: 71.8 us -> 66.6 us (0.928)
  the two profiles are of different devices: /device:TPU:1 before, /device:TPU:9 now
where the time goes in v4:
time: 66.6 us; the launch traced here: 66.4 us
  Pallas kernels  65.6 us (98%)
  between operations  0.82 us (1%)
    pallas_call x1, Pallas kernels, body(): pl.pallas_call(window_kernel, out_shape=[shape((row_count, col_count), F3...  61.8 us
    pallas_call x1, Pallas kernels, body(): pl.pallas_call(apply_kernel, out_shape=[shape((row_count, col_count), F32...  3.84 us

profile of v4, /device:TPU:9, one launch (start us, length us, event | category | flops | bytes accessed | tf_op | source)
XLA Modules:
  0.0 66.4 jit_solution(10050646585930347439)
XLA Ops:
  0.6 61.8 %window.1 = (f32[512,1024]{1,0:T(8,128)}, bf16[512,256]{1,0:T(8,128)(2,1)}, bf16[1024,256]{1,0:T(8,128)(2,1)}, f32[32,512]{1,0:T(8,128)}, f32[1,512]{1,0:T(1,128)}) custom-call(bf16[32,256]{1,0:T(8,128)(2,1)} %chunk_in.1, f32[512,1024]{1,0:T(8,128)} %whole.1, f32[1,256]{1,0:T(1,128)} %bitcast.2, s32[2,256]{1,0:T(2,128)} %orders_in.1), custom_call_target="tpu_custom_call" | custom-call | tf_op jit(solution)/shard_map/window/pallas_call | solution.py:856
  62.4 3.8 %apply.1 = (f32[512,1024]{1,0:T(8,128)}, f32[32,512]{1,0:T(8,128)}, f32[1,512]{1,0:T(1,128)}) custom-call(f32[512,1024]{1,0:T(8,128)} %get-tuple-element.11.front, bf16[512,256]{1,0:T(8,128)(2,1)} %get-tuple-element.12.new_left, bf16[1024,256]{1,0:T(8,128)(2,1)} %get-tuple-element.13.new_right, f32[32,512]{1,0:T(8,128)} %get-tuple-element.14.panels, ...), custom_call_target="tpu_custom_call" | custom-call | tf_op jit(solution)/shard_map/apply/pallas_call | solution.py:909

commit v5 on v4

--- a/solution.py
+++ b/solution.py
@@ -677,15 +677,15 @@
             handed(1, 1, to).start()
             handed(0, 1, to).start()
         second[...] = right[0:CHUNK, :]
+        with jax.named_scope("arrive"):
+            new.columns_arrive()
+
+        @pl.when(g == 1)
+        def _():
+            new.columns_send()
+
         with jax.named_scope("apply_old"):
             apply_old()
-        with jax.named_scope("arrive"):
-            new.columns_arrive()
-
-        @pl.when(g == 1)
-        def _():
-            new.columns_send()
-
         new_cols[lo, :] = jnp.zeros((WIDTH, WIDTH), BF16)
         new_cols[hi, :] = edge
         keep_near.start()

time: 66.6 us -> 66.6 us (level)
  no operation moved by 1% of the time
where the time goes in v5:
time: 66.6 us; the launch traced here: 66.4 us
  Pallas kernels  65.6 us (98%)
  between operations  0.82 us (1%)
    pallas_call x1, Pallas kernels, body(): pl.pallas_call(window_kernel, out_shape=[shape((row_count, col_count), F3...  61.8 us
    pallas_call x1, Pallas kernels, body(): pl.pallas_call(apply_kernel, out_shape=[shape((row_count, col_count), F32...  3.84 us

profile of v5, /device:TPU:9, one launch (start us, length us, event | category | flops | bytes accessed | tf_op | source)
XLA Modules:
  0.0 66.4 jit_solution(7288878240538137610)
XLA Ops:
  0.6 61.8 %window.1 = (f32[512,1024]{1,0:T(8,128)}, bf16[512,256]{1,0:T(8,128)(2,1)}, bf16[1024,256]{1,0:T(8,128)(2,1)}, f32[32,512]{1,0:T(8,128)}, f32[1,512]{1,0:T(1,128)}) custom-call(bf16[32,256]{1,0:T(8,128)(2,1)} %chunk_in.1, f32[512,1024]{1,0:T(8,128)} %whole.1, f32[1,256]{1,0:T(1,128)} %bitcast.2, s32[2,256]{1,0:T(2,128)} %orders_in.1), custom_call_target="tpu_custom_call" | custom-call | tf_op jit(solution)/shard_map/window/pallas_call | solution.py:856
  62.4 3.8 %apply.1 = (f32[512,1024]{1,0:T(8,128)}, f32[32,512]{1,0:T(8,128)}, f32[1,512]{1,0:T(1,128)}) custom-call(f32[512,1024]{1,0:T(8,128)} %get-tuple-element.11.front, bf16[512,256]{1,0:T(8,128)(2,1)} %get-tuple-element.12.new_left, bf16[1024,256]{1,0:T(8,128)(2,1)} %get-tuple-element.13.new_right, f32[32,512]{1,0:T(8,128)} %get-tuple-element.14.panels, ...), custom_call_target="tpu_custom_call" | custom-call | tf_op jit(solution)/shard_map/apply/pallas_call | solution.py:909
